TPU v7x, 32 devices: a whole 2x2x4 slice. The times are simulated.
32 devices in a mesh: face: 2 (over y), fy: 4 (over x, core), fx: 4 (over z).
Axes of the slice: x: 2, y: 2, z: 4, core: 2. Of those that a mesh axis runs over, the one named last changes fastest.
Arguments:
- state: float32 [6, 32, 32, 192], P('face', 'fy', 'fx'), may hold values from -6 to 6
- jacobian: float32 [6, 32, 32], P('face', 'fy', 'fx'), may hold values from 0.5 to 2
- metric_diag: float32 [2, 6, 32, 32], P(None, 'face', 'fy', 'fx'), may hold values from 0.6 to 1.4
- metric_cross: float32 [6, 32, 32], P('face', 'fy', 'fx'), may hold values from -0.3 to 0.3
- coriolis: float32 [6, 32, 32], P('face', 'fy', 'fx'), may hold values from -2 to 2
- nbr_face: int32 [6, 4], replicated, may hold values from 0 to 5, as said below
- nbr_edge: int32 [6, 4], replicated, may hold values from 0 to 3, as said below
Outputs:
- updated: float32 [6, 32, 32, 192], P('face', 'fy', 'fx')
Inputs may be any that keep to these rules, and one draw needn't show every extreme that they name: Edge e of a face is 0 south (row 0), 1 east (last column), 2 north (last row), 3 west (column 0). Edge e of face f is glued to edge nbr_edge[f, e] of face nbr_face[f, e], and that edge back to it; the 6 faces are glued as the surface of a cube, three faces at each corner, the two glued edges running in opposite senses when both are read counterclockwise. `nbr_edge`: see nbr_face.
All inputs are finite; a program needn't handle non-finite values.
Results may differ from a plain program's by a relative error of at most 0.0001.
Values sent between devices are 32-bit elements; how exact they have to be, the bound alone decides.
A program may use at most 64 MiB of HBM per device.

v0:
```python
import jax
import jax.numpy as jnp
import numpy as np
from jax import lax
from jax.sharding import PartitionSpec as P

time_step = 0.05
hyper_coeff = 0.0005


def padded(cells, sides, width):
    for axis, dim in sides:
        count = lax.axis_size(axis)
        ends = count - 1
        head = lax.slice_in_dim(cells, 0, width, axis=dim)
        tail = lax.slice_in_dim(cells, cells.shape[dim] - width, cells.shape[dim], axis=dim)
        cells = jnp.concatenate(
            [
                lax.ppermute(tail, axis, [(i, (i + 1) % count) for i in range(ends)]),
                cells,
                lax.ppermute(head, axis, [((i + 1) % count, i) for i in range(ends)]),
            ],
            axis=dim,
        )
    return cells


def deriv_table():
    gll_nodes = np.array([-1.0, -1.0 / np.sqrt(5.0), 1.0 / np.sqrt(5.0), 1.0])
    bary_weights = np.ones(4)
    for j in range(4):
        for m in range(4):
            if m != j:
                bary_weights[j] = bary_weights[j] / (gll_nodes[j] - gll_nodes[m])
    matrix = np.zeros((4, 4))
    for i in range(4):
        for j in range(4):
            if i != j:
                matrix[i, j] = bary_weights[j] / bary_weights[i] / (gll_nodes[i] - gll_nodes[j])
        matrix[i, i] = -np.sum(matrix[i])
    return matrix


def along_x(values):
    face_count, row_count, col_count, chan_count = values.shape
    blocks = values.reshape(face_count, row_count, col_count // 4, 4, chan_count)
    result = jnp.einsum(
        "jk,abekc->abejc",
        jnp.asarray(deriv_table(), jnp.float32),
        blocks,
        precision=lax.Precision.HIGHEST,
    )
    return result.reshape(values.shape)


def along_y(values):
    face_count, row_count, col_count, chan_count = values.shape
    blocks = values.reshape(face_count, row_count // 4, 4, col_count, chan_count)
    result = jnp.einsum(
        "ik,aekxc->aeixc",
        jnp.asarray(deriv_table(), jnp.float32),
        blocks,
        precision=lax.Precision.HIGHEST,
    )
    return result.reshape(values.shape)


def mass_of(jacobian):
    weights = jnp.asarray([1.0 / 6.0, 5.0 / 6.0, 5.0 / 6.0, 1.0 / 6.0], jnp.float32)
    row_weight = jnp.tile(weights, jacobian.shape[1] // 4)
    col_weight = jnp.tile(weights, jacobian.shape[2] // 4)
    return jacobian * row_weight[None, :, None] * col_weight[None, None, :]


def tendency(state, geometry, planet):
    volume, metric_xx, metric_yy, metric_xy = geometry
    levels = state.shape[-1] // 3
    wind_u = state[..., :levels]
    wind_v = state[..., levels : 2 * levels]
    temper = state[..., 2 * levels :]
    contra_u = metric_xx * wind_u + metric_xy * wind_v
    contra_v = metric_xy * wind_u + metric_yy * wind_v
    energy = 0.5 * (wind_u * contra_u + wind_v * contra_v) + temper
    xderivs = along_x(jnp.concatenate([wind_v, temper, energy], -1))
    yderivs = along_y(jnp.concatenate([wind_u, temper, energy], -1))
    absolute = (xderivs[..., :levels] - yderivs[..., :levels]) / volume + planet
    tend_u = absolute * volume * contra_v - xderivs[..., 2 * levels :]
    tend_v = -absolute * volume * contra_u - yderivs[..., 2 * levels :]
    tend_t = -(
        contra_u * xderivs[..., levels : 2 * levels] + contra_v * yderivs[..., levels : 2 * levels]
    )
    return state + time_step * jnp.concatenate([tend_u, tend_v, tend_t], -1)


def laplace(values, geometry):
    volume, metric_xx, metric_yy, metric_xy = geometry
    grad_x = along_x(values)
    grad_y = along_y(values)
    flux_x = volume * (metric_xx * grad_x + metric_xy * grad_y)
    flux_y = volume * (metric_xy * grad_x + metric_yy * grad_y)
    return (along_x(flux_x) + along_y(flux_y)) / volume


def combine(values, axis):
    length = values.shape[axis] - 2
    positions = jnp.arange(length)
    leading = (positions % 4 == 0).astype(jnp.float32)
    trailing = (positions % 4 == 3).astype(jnp.float32)
    broad_shape = [1, 1, 1, 1]
    broad_shape[axis] = length
    leading = leading.reshape(broad_shape)
    trailing = trailing.reshape(broad_shape)
    middle = lax.slice_in_dim(values, 1, length + 1, axis=axis)
    previous = lax.slice_in_dim(values, 0, length, axis=axis)
    following = lax.slice_in_dim(values, 2, length + 2, axis=axis)
    return middle + leading * previous + trailing * following


def rotate(segment, quarter, levels):
    cosine = ((quarter == 0).astype(jnp.float32) - (quarter == 2).astype(jnp.float32))[..., None]
    sine_part = ((quarter == 1).astype(jnp.float32) - (quarter == 3).astype(jnp.float32))[..., None]
    wind_u = segment[..., :levels]
    wind_v = segment[..., levels : 2 * levels]
    return jnp.concatenate(
        [
            cosine * wind_u - sine_part * wind_v,
            sine_part * wind_u + cosine * wind_v,
            segment[..., 2 * levels :],
        ],
        -1,
    )


def in_face(values):
    across = combine(padded(values, (("fx", 2),), 1), 2)
    return combine(padded(across, (("fy", 1),), 1), 1)


def place_pieces(
    got_flat,
    got_tall,
    vector,
    nbr_edge,
    flat_edge,
    tall_edge,
    on_south,
    on_west,
    flat_start,
    tall_start,
    face_local,
    side_nodes,
    chan_count,
    levels,
):
    edge_ids = jnp.arange(4, dtype=jnp.int32)
    flat_target = nbr_edge[:, flat_edge]
    tall_target = nbr_edge[:, tall_edge]
    if vector:
        got_flat = rotate(got_flat, ((flat_target - flat_edge + 2) % 4)[None, :, None], levels)
        got_tall = rotate(got_tall, ((tall_target - tall_edge + 2) % 4)[None, :, None], levels)
    got_flat = jnp.where(on_south, got_flat[:, :, ::-1], got_flat)
    got_tall = jnp.where(on_west, got_tall, got_tall[:, :, ::-1])
    flat_pick = (flat_target[:, None] == edge_ids[None, :]).astype(jnp.float32)
    tall_pick = (tall_target[:, None] == edge_ids[None, :]).astype(jnp.float32)
    flat_rims = jnp.einsum("se,gsjc->gejc", flat_pick, got_flat, precision=lax.Precision.HIGHEST)
    tall_rims = jnp.einsum("se,gsjc->gejc", tall_pick, got_tall, precision=lax.Precision.HIGHEST)
    empty_rims = jnp.zeros((face_local, 4, side_nodes, chan_count), jnp.float32)
    rim_strips = lax.dynamic_update_slice(empty_rims, flat_rims, (0, 0, flat_start, 0))
    return rim_strips + lax.dynamic_update_slice(empty_rims, tall_rims, (0, 0, tall_start, 0))


def outgoing(
    summed, nbr_face, face_ids, flat_edge, tall_edge, on_south, on_west, flat_live, tall_live
):
    row_count = summed.shape[1]
    col_count = summed.shape[2]
    all_faces = jnp.arange(nbr_face.shape[0], dtype=jnp.int32)
    flat_piece = jnp.where(on_south, summed[:, 0], summed[:, row_count - 1])
    tall_piece = jnp.where(on_west, summed[:, :, 0], summed[:, :, col_count - 1])
    flat_dest = nbr_face[face_ids, flat_edge]
    tall_dest = nbr_face[face_ids, tall_edge]
    flat_send = ((all_faces[:, None] == flat_dest[None, :]) & flat_live).astype(jnp.float32)
    tall_send = ((all_faces[:, None] == tall_dest[None, :]) & tall_live).astype(jnp.float32)
    return (
        flat_send[:, :, None, None] * flat_piece[None],
        tall_send[:, :, None, None] * tall_piece[None],
    )


def assemble(values, vector, nbr_face, nbr_edge):
    summed = in_face(values)
    face_local, row_count, col_count, chan_count = summed.shape
    levels = chan_count // 3
    row_index = lax.axis_index("fy")
    col_index = lax.axis_index("fx")
    side_nodes = row_count * lax.axis_size("fy")
    face_ids = lax.axis_index("face") * face_local + jnp.arange(face_local, dtype=jnp.int32)
    on_south = row_index == 0
    on_north = row_index == lax.axis_size("fy") - 1
    on_west = col_index == 0
    on_east = col_index == lax.axis_size("fx") - 1
    flat_live = on_south | on_north
    tall_live = on_west | on_east
    flat_edge = jnp.where(on_south, 0, 2).astype(jnp.int32)
    tall_edge = jnp.where(on_west, 3, 1).astype(jnp.int32)
    flat_start = jnp.where(
        on_south, side_nodes - (col_index + 1) * col_count, col_index * col_count
    )
    tall_start = jnp.where(on_west, row_index * row_count, side_nodes - (row_index + 1) * row_count)
    send_flat, send_tall = outgoing(
        summed, nbr_face, face_ids, flat_edge, tall_edge, on_south, on_west, flat_live, tall_live
    )
    got_flat, got_tall = (
        lax.all_to_all(send_flat, "face", split_axis=0, concat_axis=1, tiled=True),
        lax.all_to_all(send_tall, "face", split_axis=0, concat_axis=1, tiled=True),
    )
    rim_strips = place_pieces(
        got_flat,
        got_tall,
        vector,
        nbr_edge,
        flat_edge,
        tall_edge,
        on_south,
        on_west,
        flat_start,
        tall_start,
        face_local,
        side_nodes,
        chan_count,
        levels,
    )
    flat_lines = jnp.stack([rim_strips[:, 0], rim_strips[:, 2, ::-1]], axis=1)
    flat_lines = flat_lines.reshape(face_local, 2, lax.axis_size("fx"), col_count, chan_count)
    tall_lines = jnp.stack([rim_strips[:, 1], rim_strips[:, 3, ::-1]], axis=1)
    tall_lines = tall_lines.reshape(face_local, 2, lax.axis_size("fy"), row_count, chan_count)
    flat_whole = lax.psum(flat_lines, "fy")
    tall_whole = lax.psum(tall_lines, "fx")
    flat_block = lax.psum_scatter(flat_whole, "fx", scatter_dimension=2, tiled=True)
    tall_block = lax.psum_scatter(tall_whole, "fy", scatter_dimension=2, tiled=True)
    flat_add = jnp.where(on_south, flat_block[:, 0, 0], flat_block[:, 1, 0])
    tall_add = jnp.where(on_west, tall_block[:, 1, 0], tall_block[:, 0, 0])
    result = summed.at[:, 0].add(jnp.where(on_south, flat_add, 0.0))
    result = result.at[:, row_count - 1].add(jnp.where(on_north, flat_add, 0.0))
    result = result.at[:, :, 0].add(jnp.where(on_west, tall_add, 0.0))
    result = result.at[:, :, col_count - 1].add(jnp.where(on_east, tall_add, 0.0))
    return result


def per_device(state, jacobian, metric_diag, metric_cross, coriolis, nbr_face, nbr_edge):
    node_mass = mass_of(jacobian)[..., None]
    total_mass = assemble(node_mass, False, nbr_face, nbr_edge)
    geometry = (
        jacobian[..., None],
        metric_diag[0][..., None],
        metric_diag[1][..., None],
        metric_cross[..., None],
    )
    raw = tendency(state, geometry, coriolis[..., None])
    sectioned = assemble(node_mass * raw, True, nbr_face, nbr_edge) / total_mass
    first_lap = (
        assemble(node_mass * laplace(sectioned, geometry), True, nbr_face, nbr_edge) / total_mass
    )
    second_lap = (
        assemble(node_mass * laplace(first_lap, geometry), True, nbr_face, nbr_edge) / total_mass
    )
    return sectioned - hyper_coeff * second_lap


def solution(mesh):
    return jax.shard_map(
        per_device,
        mesh=mesh,
        in_specs=(
            P("face", "fy", "fx", None),
            P("face", "fy", "fx"),
            P(None, "face", "fy", "fx"),
            P("face", "fy", "fx"),
            P("face", "fy", "fx"),
            P(),
            P(),
        ),
        out_specs=P("face", "fy", "fx", None),
        check_vma=False,
    )
```

profile of v0, /device:TPU:0, one launch (start us, length us, event | category | flops | bytes accessed | tf_op | source)
XLA Modules:
  0.0 370.9 jit_solution(3466996314126042414)
XLA Ops:
  7.4 0.8 fusion.161
  8.1 1.0 slice.770
  13.0 1.3 collective-permute-start.1
  14.4 5.6 %collective-permute-start = (f32[3,8,1,192]{3,2,0,1:T(1,128)S(1)}, f32[3,8,1,192]{3,2,0,1:T(1,128)S(1)}, u32[]{:S(2)}, u32[]{:S(2)}) collective-permute-start(f32[3,8,1,192]{3,2,0,1:T(1,128)S(1)} %slice.902), channel_id=1, source_target_pairs={{0,1},{1,2},{2,3},{4,5},{5,6},{6,7},{8,9},{9,10},{10,11},{12,13},{... | collective-permute-start | bytes 55304 | tf_op jit(solution)/shard_map/ppermute | solution.py:19
  20.1 1.3 collective-permute-start.5
  21.4 4.5 %collective-permute-start.4 = (f32[3,8,1,1]{2,1,0,3:T(8,128)S(1)}, f32[3,8,1,1]{2,1,0,3:T(8,128)S(1)}, u32[]{:S(2)}, u32[]{:S(2)}) collective-permute-start(f32[3,8,1,1]{2,1,0,3:T(8,128)S(1)} %get-tuple-element.262), channel_id=1, source_target_pairs={{0,1},{1,2},{2,3},{4,5},{5,6},{6,7},{8,9},{9,10},{10,11},{12,13},{... | collective-permute-start | bytes 296 | tf_op jit(solution)/shard_map/ppermute | solution.py:19
  31.1 1.3 collective-permute-start.7
  32.4 3.0 collective-permute-start.6
  35.5 0.8 collective-permute-done.6
  37.2 3.2 all-to-all-start.2
  41.1 3.1 all-to-all-done.2
  44.3 3.2 all-to-all-start.3
  47.6 3.7 all-to-all-done.3
  52.8 1.3 collective-permute-start.3
  54.1 3.0 collective-permute-start.2
  57.2 13.3 %all-reduce.4 = f32[3,2,4,8,1]{3,1,4,0,2:T(2,128)S(1)} all-reduce(f32[3,2,4,8,1]{3,1,4,0,2:T(2,128)S(1)} %copy.284), channel_id=5, replica_groups=mesh['face'=2,'fy'=4,'fx'=4] {'fy'}, use_global_device_ids=true, to_apply=%region_7.8.clone | all-reduce | flops 192 | bytes 1536
  70.7 0.7 broadcast_multiply_fusion.5
  71.4 3.4 all-to-all-start
  74.9 0.8 broadcast_multiply_fusion.4
  75.7 3.7 %all-to-all-done = f32[6,3,8,192]{3,2,1,0:T(8,128)S(1)} async-done(((f32[6,3,8,192]{3,2,1,0:T(8,128)}), f32[6,3,8,192]{3,2,1,0:T(8,128)S(1)}, u32[]{:S(2)}, u32[]{:S(2)}) %all-to-all-start) | async-done | bytes 110624 | tf_op jit(solution)/shard_map/all_to_all | solution.py:214
  79.4 3.4 all-to-all-start.1
  83.3 4.1 %all-to-all-done.1 = f32[6,3,8,192]{3,2,1,0:T(8,128)S(1)} async-done(((f32[6,3,8,192]{3,2,1,0:T(8,128)}), f32[6,3,8,192]{3,2,1,0:T(8,128)S(1)}, u32[]{:S(2)}, u32[]{:S(2)}) %all-to-all-start.1) | async-done | bytes 110624 | tf_op jit(solution)/shard_map/all_to_all | solution.py:215
  88.9 0.7 copy.270
  91.5 33.0 %all-reduce.13.cloned.1.call-done = f32[3,2,4,8,192]{4,3,0,2,1:T(8,128)} async-done(((f32[3,2,4,8,192]{4,3,0,2,1:T(8,128)}), f32[3,2,4,8,192]{4,3,0,2,1:T(8,128)}) %all-reduce.13.cloned.1.call-update) | async-done | bytes 147472
  124.5 1.4 constant_dynamic-slice_fusion.6
  125.9 0.8 copy.277
  126.8 18.5 %all-reduce.7 = (f32[3,2,1,8,192]{4,1,3,2,0:T(2,128)S(1)}, f32[3,2,4,8,1]{3,1,4,0,2:T(2,128)S(1)}, f32[3,2,1,8,1]{3,1,4,0,2:T(2,128)S(1)}) all-reduce(f32[3,2,1,8,192]{4,1,3,2,0:T(2,128)S(1)} %copy.277, f32[3,2,4,8,1]{3,1,4,0,2:T(2,128)S(1)} %copy.281, ...), channel_id=1, replica_groups=mesh['face'=2,'fy'=4,'fx'=4] {'fx'}, use_global_device_ids=true, to_apply=%region_2.3 | all-reduce | flops 9456 | bytes 75648 | tf_op jit(solution)/shard_map/psum | solution.py:238
  145.9 10.7 %all-reduce.8 = (f32[3,2,1,8,192]{4,3,0,2,1:T(8,128)S(1)}, f32[3,2,1,8,1]{3,1,4,0,2:T(2,128)S(1)}) all-reduce(f32[3,2,1,8,192]{4,3,0,2,1:T(8,128)S(1)} %constant_dynamic-slice_fusion.6, f32[3,2,1,8,1]{3,1,4,0,2:T(2,128)S(1)} %constant_dynamic-slice_fusion.5), channel_id=1, replica_groups=mesh['face'=2,'fy'=4,'fx'=4] {'fy'}, use_global_device_ids=true, to_apply=%region_0.1 | all-reduce | flops 9264 | bytes 74112 | tf_op jit(solution)/shard_map/psum | solution.py:237
  160.6 1.3 collective-permute-start.9
  161.9 4.5 %collective-permute-start.8 = (f32[3,8,1,192]{3,2,0,1:T(1,128)S(1)}, f32[3,8,1,192]{3,2,0,1:T(1,128)S(1)}, u32[]{:S(2)}, u32[]{:S(2)}) collective-permute-start(f32[3,8,1,192]{3,2,0,1:T(1,128)S(1)} %get-tuple-element.230), channel_id=1, source_target_pairs={{0,1},{1,2},{2,3},{4,5},{5,6},{6,7},{8,9},{9,10},{10,11},{12,13},{... | collective-permute-start | bytes 55304 | tf_op jit(solution)/shard_map/ppermute | solution.py:19
  166.4 1.5 collective-permute-done.8
  168.0 1.3 collective-permute-start.11
  169.3 3.2 collective-permute-start.10
  173.4 0.7 broadcast_multiply_fusion.3
  174.1 3.4 all-to-all-start.4
  177.6 0.8 broadcast_multiply_fusion.2
  178.3 4.0 %all-to-all-done.4 = f32[6,3,8,192]{3,2,1,0:T(8,128)S(1)} async-done(((f32[6,3,8,192]{3,2,1,0:T(8,128)}), f32[6,3,8,192]{3,2,1,0:T(8,128)S(1)}, u32[]{:S(2)}, u32[]{:S(2)}) %all-to-all-start.4) | async-done | bytes 110624 | tf_op jit(solution)/shard_map/all_to_all | solution.py:214
  182.3 3.4 all-to-all-start.5
  186.2 4.3 %all-to-all-done.5 = f32[6,3,8,192]{3,2,1,0:T(8,128)S(1)} async-done(((f32[6,3,8,192]{3,2,1,0:T(8,128)}), f32[6,3,8,192]{3,2,1,0:T(8,128)S(1)}, u32[]{:S(2)}, u32[]{:S(2)}) %all-to-all-start.5) | async-done | bytes 110624 | tf_op jit(solution)/shard_map/all_to_all | solution.py:215
  192.1 0.7 copy.308
  193.8 35.0 %all-reduce.15.cloned.1.call-done = f32[3,2,4,8,192]{4,3,0,2,1:T(8,128)} async-done(((f32[3,2,4,8,192]{4,3,0,2,1:T(8,128)}), f32[3,2,4,8,192]{4,3,0,2,1:T(8,128)}) %all-reduce.15.cloned.1.call-update) | async-done | bytes 147472
  228.8 1.4 constant_dynamic-slice_fusion.3
  230.3 10.5 %psum.68 = f32[3,2,1,8,192]{4,3,0,2,1:T(8,128)S(1)} all-reduce(f32[3,2,1,8,192]{4,3,0,2,1:T(8,128)S(1)} %constant_dynamic-slice_fusion.3), channel_id=1, replica_groups=mesh['face'=2,'fy'=4,'fx'=4] {'fy'}, use_global_device_ids=true, to_apply=%region_8.9 | all-reduce | flops 9216 | bytes 73728 | tf_op jit(solution)/shard_map/psum | solution.py:237
  240.9 0.8 copy.314
  241.7 18.2 %psum.69 = f32[3,2,1,8,192]{4,1,3,2,0:T(2,128)S(1)} all-reduce(f32[3,2,1,8,192]{4,1,3,2,0:T(2,128)S(1)} %copy.314), channel_id=1, replica_groups=mesh['face'=2,'fy'=4,'fx'=4] {'fx'}, use_global_device_ids=true, to_apply=%region_10.11 | all-reduce | flops 9216 | bytes 73728 | tf_op jit(solution)/shard_map/psum | solution.py:238
  263.2 1.3 collective-permute-start.13
  264.5 4.5 %collective-permute-start.12 = (f32[3,8,1,192]{3,2,0,1:T(1,128)S(1)}, f32[3,8,1,192]{3,2,0,1:T(1,128)S(1)}, u32[]{:S(2)}, u32[]{:S(2)}) collective-permute-start(f32[3,8,1,192]{3,2,0,1:T(1,128)S(1)} %get-tuple-element.226), channel_id=1, source_target_pairs={{0,1},{1,2},{2,3},{4,5},{5,6},{6,7},{8,9},{9,10},{10,11},{12,13},{... | collective-permute-start | bytes 55304 | tf_op jit(solution)/shard_map/ppermute | solution.py:19
  269.0 1.5 collective-permute-done.12
  270.6 1.3 collective-permute-start.15
  271.9 3.0 collective-permute-start.14
  275.0 0.8 collective-permute-done.14
  276.0 0.7 broadcast_multiply_fusion.1
  276.7 3.4 all-to-all-start.6
  280.2 0.8 broadcast_multiply_fusion
  280.9 4.0 %all-to-all-done.6 = f32[6,3,8,192]{3,2,1,0:T(8,128)S(1)} async-done(((f32[6,3,8,192]{3,2,1,0:T(8,128)}), f32[6,3,8,192]{3,2,1,0:T(8,128)S(1)}, u32[]{:S(2)}, u32[]{:S(2)}) %all-to-all-start.6) | async-done | bytes 110624 | tf_op jit(solution)/shard_map/all_to_all | solution.py:214
  284.9 3.4 all-to-all-start.7
  288.9 4.2 %all-to-all-done.7 = f32[6,3,8,192]{3,2,1,0:T(8,128)S(1)} async-done(((f32[6,3,8,192]{3,2,1,0:T(8,128)}), f32[6,3,8,192]{3,2,1,0:T(8,128)S(1)}, u32[]{:S(2)}, u32[]{:S(2)}) %all-to-all-start.7) | async-done | bytes 110624 | tf_op jit(solution)/shard_map/all_to_all | solution.py:215
  294.7 0.7 copy.326
  296.4 34.9 %all-reduce.17.cloned.1.call-done = f32[3,2,4,8,192]{4,3,0,2,1:T(8,128)} async-done(((f32[3,2,4,8,192]{4,3,0,2,1:T(8,128)}), f32[3,2,4,8,192]{4,3,0,2,1:T(8,128)}) %all-reduce.17.cloned.1.call-update) | async-done | bytes 147472
  331.3 1.4 constant_dynamic-slice_fusion.2
  332.8 10.5 %psum.70 = f32[3,2,1,8,192]{4,3,0,2,1:T(8,128)S(1)} all-reduce(f32[3,2,1,8,192]{4,3,0,2,1:T(8,128)S(1)} %constant_dynamic-slice_fusion.2), channel_id=1, replica_groups=mesh['face'=2,'fy'=4,'fx'=4] {'fy'}, use_global_device_ids=true, to_apply=%region_12.13 | all-reduce | flops 9216 | bytes 73728 | tf_op jit(solution)/shard_map/psum | solution.py:237
  343.4 0.8 copy.330
  344.2 18.2 %psum.71 = f32[3,2,1,8,192]{4,1,3,2,0:T(2,128)S(1)} all-reduce(f32[3,2,1,8,192]{4,1,3,2,0:T(2,128)S(1)} %copy.330), channel_id=1, replica_groups=mesh['face'=2,'fy'=4,'fx'=4] {'fx'}, use_global_device_ids=true, to_apply=%region_14.15 | all-reduce | flops 9216 | bytes 73728 | tf_op jit(solution)/shard_map/psum | solution.py:238
  362.8 0.8 multiply_subtract_fusion
  (252 shorter events, 31.3 us)
Async XLA Ops:
  7.4 19.6 %copy-start = (s32[6,4]{0,1:T(4,128)S(1)}, s32[6,4]{0,1:T(4,128)}, u32[]{:S(2)}) copy-start(s32[6,4]{0,1:T(4,128)} %param.55) | copy-start | bytes 292
  7.4 1.8 copy-start.1
  8.1 1.0 copy-start.3
  9.5 0.7 copy-start.4
  11.2 0.7 copy-start.9
  11.2 0.7 copy-start.2
  12.0 0.7 copy-start.5
  13.0 39.6 %collective-permute-start.1 = (f32[3,8,1,192]{3,2,1,0:T(1,128)S(1)}, f32[3,8,1,192]{3,2,1,0:T(1,128)S(1)}, u32[]{:S(2)}, u32[]{:S(2)}) collective-permute-start(f32[3,8,1,192]{3,2,1,0:T(1,128)S(1)} %slice.903), channel_id=1, source_target_pairs={{1,0},{2,1},{3,2},{5,4},{6,5},{7,6},{9,8},{10,9},{11,10},{13,12},{... | collective-permute-start | bytes 55304 | tf_op jit(solution)/shard_map/ppermute | solution.py:21
  14.4 38.2 %collective-permute-start = (f32[3,8,1,192]{3,2,0,1:T(1,128)S(1)}, f32[3,8,1,192]{3,2,0,1:T(1,128)S(1)}, u32[]{:S(2)}, u32[]{:S(2)}) collective-permute-start(f32[3,8,1,192]{3,2,0,1:T(1,128)S(1)} %slice.902), channel_id=1, source_target_pairs={{0,1},{1,2},{2,3},{4,5},{5,6},{6,7},{8,9},{9,10},{10,11},{12,13},{... | collective-permute-start | bytes 55304 | tf_op jit(solution)/shard_map/ppermute | solution.py:19
  20.1 10.9 %collective-permute-start.5 = (f32[3,8,1,1]{2,1,0,3:T(8,128)S(1)}, f32[3,8,1,1]{2,1,0,3:T(8,128)S(1)}, u32[]{:S(2)}, u32[]{:S(2)}) collective-permute-start(f32[3,8,1,1]{2,1,0,3:T(8,128)S(1)} %get-tuple-element.263), channel_id=1, source_target_pairs={{1,0},{2,1},{3,2},{5,4},{6,5},{7,6},{9,8},{10,9},{11,10},{13,12},{... | collective-permute-start | bytes 296 | tf_op jit(solution)/shard_map/ppermute | solution.py:21
  21.4 9.6 %collective-permute-start.4 = (f32[3,8,1,1]{2,1,0,3:T(8,128)S(1)}, f32[3,8,1,1]{2,1,0,3:T(8,128)S(1)}, u32[]{:S(2)}, u32[]{:S(2)}) collective-permute-start(f32[3,8,1,1]{2,1,0,3:T(8,128)S(1)} %get-tuple-element.262), channel_id=1, source_target_pairs={{0,1},{1,2},{2,3},{4,5},{5,6},{6,7},{8,9},{9,10},{10,11},{12,13},{... | collective-permute-start | bytes 296 | tf_op jit(solution)/shard_map/ppermute | solution.py:19
  26.0 0.7 copy-start.6
  28.3 0.7 copy-start.8
  28.9 0.7 copy-start.7
  31.1 4.3 %collective-permute-start.7 = (f32[3,1,8,1]{2,1,0,3:T(1,128)S(1)}, f32[3,1,8,1]{2,1,0,3:T(1,128)S(1)}, u32[]{:S(2)}, u32[]{:S(2)}) collective-permute-start(f32[3,1,8,1]{2,1,0,3:T(1,128)S(1)} %get-tuple-element.261), channel_id=1, source_target_pairs={{4,0},{8,4},{12,8},{5,1},{9,5},{13,9},{6,2},{10,6},{14,10},{7,3},{... | collective-permute-start | bytes 296 | tf_op jit(solution)/shard_map/ppermute | solution.py:21
  32.4 3.8 %collective-permute-start.6 = (f32[3,1,8,1]{2,1,0,3:T(1,128)S(1)}, f32[3,1,8,1]{2,1,0,3:T(1,128)S(1)}, u32[]{:S(2)}, u32[]{:S(2)}) collective-permute-start(f32[3,1,8,1]{2,1,0,3:T(1,128)S(1)} %get-tuple-element.260), channel_id=1, source_target_pairs={{0,4},{4,8},{8,12},{1,5},{5,9},{9,13},{2,6},{6,10},{10,14},{3,7},{... | collective-permute-start | bytes 296 | tf_op jit(solution)/shard_map/ppermute | solution.py:19
  37.2 7.0 %all-to-all-start.2 = ((f32[6,3,8,1]{2,3,1,0:T(1,128)}), f32[6,3,8,1]{2,3,1,0:T(1,128)S(1)}, u32[]{:S(2)}, u32[]{:S(2)}) async-start(f32[6,3,8,1]{2,3,1,0:T(1,128)} %broadcast_multiply_fusion.7), calls=%async_computation.2 | async-start | bytes 18432 | tf_op jit(solution)/shard_map/all_to_all | solution.py:214
  44.3 7.0 %all-to-all-start.3 = ((f32[6,3,8,1]{2,3,1,0:T(1,128)}), f32[6,3,8,1]{2,3,1,0:T(1,128)S(1)}, u32[]{:S(2)}, u32[]{:S(2)}) async-start(f32[6,3,8,1]{2,3,1,0:T(1,128)} %broadcast_multiply_fusion.6), calls=%async_computation.3 | async-start | bytes 18432 | tf_op jit(solution)/shard_map/all_to_all | solution.py:215
  52.8 17.7 %collective-permute-start.3 = (f32[3,1,8,192]{3,2,1,0:T(8,128)S(1)}, f32[3,1,8,192]{3,2,1,0:T(8,128)S(1)}, u32[]{:S(2)}, u32[]{:S(2)}) collective-permute-start(f32[3,1,8,192]{3,2,1,0:T(8,128)S(1)} %slice.905), channel_id=1, source_target_pairs={{4,0},{8,4},{12,8},{5,1},{9,5},{13,9},{6,2},{10,6},{14,10},{7,3},{... | collective-permute-start | bytes 55304 | tf_op jit(solution)/shard_map/ppermute | solution.py:21
  54.1 16.4 %collective-permute-start.2 = (f32[3,1,8,192]{3,2,0,1:T(8,128)S(1)}, f32[3,1,8,192]{3,2,0,1:T(8,128)S(1)}, u32[]{:S(2)}, u32[]{:S(2)}) collective-permute-start(f32[3,1,8,192]{3,2,0,1:T(8,128)S(1)} %slice.904), channel_id=1, source_target_pairs={{0,4},{4,8},{8,12},{1,5},{5,9},{9,13},{2,6},{6,10},{10,14},{3,7},{... | collective-permute-start | bytes 55304 | tf_op jit(solution)/shard_map/ppermute | solution.py:19
  71.4 8.0 %all-to-all-start = ((f32[6,3,8,192]{3,2,1,0:T(8,128)}), f32[6,3,8,192]{3,2,1,0:T(8,128)S(1)}, u32[]{:S(2)}, u32[]{:S(2)}) async-start(f32[6,3,8,192]{3,2,1,0:T(8,128)} %broadcast_multiply_fusion.5), calls=%async_computation | async-start | bytes 294912 | tf_op jit(solution)/shard_map/all_to_all | solution.py:214
  79.4 8.0 %all-to-all-start.1 = ((f32[6,3,8,192]{3,2,1,0:T(8,128)}), f32[6,3,8,192]{3,2,1,0:T(8,128)S(1)}, u32[]{:S(2)}, u32[]{:S(2)}) async-start(f32[6,3,8,192]{3,2,1,0:T(8,128)} %broadcast_multiply_fusion.4), calls=%async_computation.1 | async-start | bytes 294912 | tf_op jit(solution)/shard_map/all_to_all | solution.py:215
  82.8 41.7 %all-reduce.13.cloned.1.call-start = ((), (), s32[]{:S(2)}) async-start(), calls=%async_computation.14 | async-start | bytes 393216
  89.7 36.3 %reduce-scatter.7.cloned.1.call-start = ((), (), s32[]{:S(2)}) async-start(), calls=%async_computation.11 | async-start | bytes 245760 | tf_op jit(solution)/shard_map/reduce_scatter | solution.py:240
  160.6 5.9 %collective-permute-start.9 = (f32[3,8,1,192]{3,2,0,1:T(1,128)S(1)}, f32[3,8,1,192]{3,2,0,1:T(1,128)S(1)}, u32[]{:S(2)}, u32[]{:S(2)}) collective-permute-start(f32[3,8,1,192]{3,2,0,1:T(1,128)S(1)} %get-tuple-element.231), channel_id=1, source_target_pairs={{1,0},{2,1},{3,2},{5,4},{6,5},{7,6},{9,8},{10,9},{11,10},{13,12},{... | collective-permute-start | bytes 55304 | tf_op jit(solution)/shard_map/ppermute | solution.py:21
  161.9 6.1 %collective-permute-start.8 = (f32[3,8,1,192]{3,2,0,1:T(1,128)S(1)}, f32[3,8,1,192]{3,2,0,1:T(1,128)S(1)}, u32[]{:S(2)}, u32[]{:S(2)}) collective-permute-start(f32[3,8,1,192]{3,2,0,1:T(1,128)S(1)} %get-tuple-element.230), channel_id=1, source_target_pairs={{0,1},{1,2},{2,3},{4,5},{5,6},{6,7},{8,9},{9,10},{10,11},{12,13},{... | collective-permute-start | bytes 55304 | tf_op jit(solution)/shard_map/ppermute | solution.py:19
  168.0 4.5 %collective-permute-start.11 = (f32[3,1,8,192]{3,2,0,1:T(8,128)S(1)}, f32[3,1,8,192]{3,2,0,1:T(8,128)S(1)}, u32[]{:S(2)}, u32[]{:S(2)}) collective-permute-start(f32[3,1,8,192]{3,2,0,1:T(8,128)S(1)} %get-tuple-element.229), channel_id=1, source_target_pairs={{4,0},{8,4},{12,8},{5,1},{9,5},{13,9},{6,2},{10,6},{14,10},{7,3},{... | collective-permute-start | bytes 55304 | tf_op jit(solution)/shard_map/ppermute | solution.py:21
  169.3 3.9 %collective-permute-start.10 = (f32[3,1,8,192]{3,2,0,1:T(8,128)S(1)}, f32[3,1,8,192]{3,2,0,1:T(8,128)S(1)}, u32[]{:S(2)}, u32[]{:S(2)}) collective-permute-start(f32[3,1,8,192]{3,2,0,1:T(8,128)S(1)} %get-tuple-element.228), channel_id=1, source_target_pairs={{0,4},{4,8},{8,12},{1,5},{5,9},{9,13},{2,6},{6,10},{10,14},{3,7},{... | collective-permute-start | bytes 55304 | tf_op jit(solution)/shard_map/ppermute | solution.py:19
  174.1 8.2 %all-to-all-start.4 = ((f32[6,3,8,192]{3,2,1,0:T(8,128)}), f32[6,3,8,192]{3,2,1,0:T(8,128)S(1)}, u32[]{:S(2)}, u32[]{:S(2)}) async-start(f32[6,3,8,192]{3,2,1,0:T(8,128)} %broadcast_multiply_fusion.3), calls=%async_computation.4 | async-start | bytes 294912 | tf_op jit(solution)/shard_map/all_to_all | solution.py:214
  182.3 8.2 %all-to-all-start.5 = ((f32[6,3,8,192]{3,2,1,0:T(8,128)}), f32[6,3,8,192]{3,2,1,0:T(8,128)S(1)}, u32[]{:S(2)}, u32[]{:S(2)}) async-start(f32[6,3,8,192]{3,2,1,0:T(8,128)} %broadcast_multiply_fusion.2), calls=%async_computation.5 | async-start | bytes 294912 | tf_op jit(solution)/shard_map/all_to_all | solution.py:215
  185.7 43.1 %all-reduce.15.cloned.1.call-start = ((), (), s32[]{:S(2)}) async-start(), calls=%async_computation.15 | async-start | bytes 393216
  192.8 48.1 %reduce-scatter.9.cloned.1.call-start = ((), (), s32[]{:S(2)}) async-start(), calls=%async_computation.12 | async-start | bytes 245760 | tf_op jit(solution)/shard_map/reduce_scatter | solution.py:240
  263.2 5.9 %collective-permute-start.13 = (f32[3,8,1,192]{3,2,0,1:T(1,128)S(1)}, f32[3,8,1,192]{3,2,0,1:T(1,128)S(1)}, u32[]{:S(2)}, u32[]{:S(2)}) collective-permute-start(f32[3,8,1,192]{3,2,0,1:T(1,128)S(1)} %get-tuple-element.227), channel_id=1, source_target_pairs={{1,0},{2,1},{3,2},{5,4},{6,5},{7,6},{9,8},{10,9},{11,10},{13,12},{... | collective-permute-start | bytes 55304 | tf_op jit(solution)/shard_map/ppermute | solution.py:21
  264.5 6.1 %collective-permute-start.12 = (f32[3,8,1,192]{3,2,0,1:T(1,128)S(1)}, f32[3,8,1,192]{3,2,0,1:T(1,128)S(1)}, u32[]{:S(2)}, u32[]{:S(2)}) collective-permute-start(f32[3,8,1,192]{3,2,0,1:T(1,128)S(1)} %get-tuple-element.226), channel_id=1, source_target_pairs={{0,1},{1,2},{2,3},{4,5},{5,6},{6,7},{8,9},{9,10},{10,11},{12,13},{... | collective-permute-start | bytes 55304 | tf_op jit(solution)/shard_map/ppermute | solution.py:19
  270.6 4.3 %collective-permute-start.15 = (f32[3,1,8,192]{3,2,0,1:T(8,128)S(1)}, f32[3,1,8,192]{3,2,0,1:T(8,128)S(1)}, u32[]{:S(2)}, u32[]{:S(2)}) collective-permute-start(f32[3,1,8,192]{3,2,0,1:T(8,128)S(1)} %get-tuple-element.225), channel_id=1, source_target_pairs={{4,0},{8,4},{12,8},{5,1},{9,5},{13,9},{6,2},{10,6},{14,10},{7,3},{... | collective-permute-start | bytes 55304 | tf_op jit(solution)/shard_map/ppermute | solution.py:21
  271.9 3.9 %collective-permute-start.14 = (f32[3,1,8,192]{3,2,0,1:T(8,128)S(1)}, f32[3,1,8,192]{3,2,0,1:T(8,128)S(1)}, u32[]{:S(2)}, u32[]{:S(2)}) collective-permute-start(f32[3,1,8,192]{3,2,0,1:T(8,128)S(1)} %get-tuple-element.224), channel_id=1, source_target_pairs={{0,4},{4,8},{8,12},{1,5},{5,9},{9,13},{2,6},{6,10},{10,14},{3,7},{... | collective-permute-start | bytes 55304 | tf_op jit(solution)/shard_map/ppermute | solution.py:19
  276.7 8.2 %all-to-all-start.6 = ((f32[6,3,8,192]{3,2,1,0:T(8,128)}), f32[6,3,8,192]{3,2,1,0:T(8,128)S(1)}, u32[]{:S(2)}, u32[]{:S(2)}) async-start(f32[6,3,8,192]{3,2,1,0:T(8,128)} %broadcast_multiply_fusion.1), calls=%async_computation.6 | async-start | bytes 294912 | tf_op jit(solution)/shard_map/all_to_all | solution.py:214
  284.9 8.2 %all-to-all-start.7 = ((f32[6,3,8,192]{3,2,1,0:T(8,128)}), f32[6,3,8,192]{3,2,1,0:T(8,128)S(1)}, u32[]{:S(2)}, u32[]{:S(2)}) async-start(f32[6,3,8,192]{3,2,1,0:T(8,128)} %broadcast_multiply_fusion), calls=%async_computation.7 | async-start | bytes 294912 | tf_op jit(solution)/shard_map/all_to_all | solution.py:215
  288.4 43.0 %all-reduce.17.cloned.1.call-start = ((), (), s32[]{:S(2)}) async-start(), calls=%async_computation.16 | async-start | bytes 393216
  295.4 48.0 %reduce-scatter.11.cloned.1.call-start = ((), (), s32[]{:S(2)}) async-start(), calls=%async_computation.13 | async-start | bytes 245760 | tf_op jit(solution)/shard_map/reduce_scatter | solution.py:240
Sparse Core Ops, SparseCore 0:
  89.8 34.6 all-reduce.12
  192.9 35.8 all-reduce.14
  295.5 35.7 all-reduce.16
Sparse Core Ops, SparseCore 1:
  92.6 19.4 reduce-scatter.6
  195.7 20.6 reduce-scatter.8
  298.3 20.6 reduce-scatter.10
where the time goes:
time: 373 us; the launch traced here: 371 us
  waiting for transfers between devices  139 us (37%)
  blocking collectives  99.7 us (27%)
  starting transfers between devices  69.1 us (19%)
  local copies, waits for them, and re-layouts  26.4 us (7%)
  between operations  16.4 us (4%)
  other arithmetic  12.6 us (3%)
  matrix products  7.16 us (2%)
    unnamed x9, waiting for transfers between devices  103 us
    psum x3, blocking collectives, assemble(): tall_whole = lax.psum(tall_lines, 'fx')  54.8 us
    psum x3, blocking collectives, assemble(): flat_whole = lax.psum(flat_lines, 'fy')  31.7 us
    ppermute x8, starting transfers between devices, padded(): lax.ppermute(tail, axis, [(i, (i + 1) % count) for i in range(ends)])  31.5 us
    all_to_all x4, waiting for transfers between devices, assemble(): lax.all_to_all(send_tall, 'face', split_axis=0, concat_axis=1, tiled=True)  16.2 us
    all_to_all x4, waiting for transfers between devices, assemble(): lax.all_to_all(send_flat, 'face', split_axis=0, concat_axis=1, tiled=True)  14.9 us
    all_to_all x4, starting transfers between devices, assemble(): lax.all_to_all(send_flat, 'face', split_axis=0, concat_axis=1, tiled=True)  13.5 us
    all_to_all x4, starting transfers between devices, assemble(): lax.all_to_all(send_tall, 'face', split_axis=0, concat_axis=1, tiled=True)  13.5 us
  transfers between devices with their start and end apart: 30, of which 16 were waited for; matrix products, arithmetic and copies ran while one was open for 5% of the time, Pallas kernels for 0%

commit v1 on v0

--- a/solution.py
+++ b/solution.py
@@ -1,11 +1,17 @@
+import functools
+
 import jax
 import jax.numpy as jnp
 import numpy as np
 from jax import lax
+from jax.experimental import pallas as pl
+from jax.experimental.pallas import tpu as pltpu
 from jax.sharding import PartitionSpec as P
 
 time_step = 0.05
 hyper_coeff = 0.0005
+MESH = pl.DeviceIdType.MESH
+ROUNDS = 3
 
 
 def padded(cells, sides, width):
@@ -267,9 +273,482 @@
     return sectioned - hyper_coeff * second_lap
 
 
+SIDE = 8
+HALF = 64
+
+
+def tile_place(edge, block, blocks):
+    return [
+        (0, block),
+        (block, blocks - 1),
+        (blocks - 1, blocks - 1 - block),
+        (blocks - 1 - block, 0),
+    ][edge]
+
+
+def kernel(
+    groups,
+    blocks,
+    nbr_face,
+    nbr_edge,
+    state,
+    jac,
+    diag,
+    cross,
+    coriolis,
+    out,
+    *scratch,
+):
+    faces = state.shape[0]
+    fields, cols, packs, got_col, got_row, got_pack, rim_0, rim_1, end_0, end_1 = (
+        scratch[i * ROUNDS : (i + 1) * ROUNDS] for i in range(10)
+    )
+    got_rim = [pair for pair in zip(rim_0, rim_1)]
+    got_end = [pair for pair in zip(end_0, end_1)]
+    (summed, inverse, flux_a, flux_b, flux_c, sem_s_near, sem_r_near, sem_s_rim, sem_r_rim, sem_s_end, sem_r_end) = scratch[
+        10 * ROUNDS :
+    ]
+    g = lax.axis_index("face")
+    y = lax.axis_index("fy")
+    x = lax.axis_index("fx")
+    last = blocks - 1
+
+    barrier = pltpu.get_barrier_semaphore()
+    for tg in range(groups):
+        for ty in range(blocks):
+            for tx in range(blocks):
+
+                @pl.when(jnp.logical_not((g == tg) & (y == ty) & (x == tx)))
+                def _():
+                    pl.semaphore_signal(barrier, inc=1, device_id=(tg, ty, tx), device_id_type=MESH)
+
+    live = ((y == 0) | (y == last), (x == 0) | (x == last))
+    edge = (jnp.where(y == 0, 0, 2), jnp.where(x == 0, 3, 1))
+    place = (jnp.where(y == 0, x, last - x), jnp.where(x == 0, last - y, y))
+    at_end = (jnp.where(y == 0, 0, SIDE - 1), jnp.where(x == 0, 0, SIDE - 1))
+    side = (jnp.where(y == 0, 0, 1), jnp.where(x == 0, 0, 1))
+    head_pack = (jnp.where(y == 0, 0, 3), jnp.where(x == 0, 2, 1))
+    tail_pack = (jnp.where(y == 0, 1, 2), jnp.where(x == 0, 0, 3))
+
+    near = [(0, -1), (0, 1), (-1, 0), (1, 0), (-1, -1), (-1, 1), (1, -1), (1, 1)]
+
+    def has(dy, dx):
+        ok = None
+        for d, at in ((dy, y), (dx, x)):
+            if d:
+                one = at > 0 if d < 0 else at < last
+                ok = one if ok is None else ok & one
+        return ok
+
+    def near_copy(rnd, n):
+        dy, dx = near[n]
+        back = near.index((-dy, -dx))
+        if dy == 0:
+            w = (dx + 1) // 2
+            src, dst = cols[rnd].at[w], got_col[rnd].at[1 - w]
+        elif dx == 0:
+            w = (dy + 1) // 2
+            src, dst = fields[rnd].at[:, :, w * (SIDE - 1)], got_row[rnd].at[1 - w]
+        else:
+            w = (dy + 1) + (dx + 1) // 2
+            src, dst = packs[rnd].at[w], got_pack[rnd].at[3 - w]
+        return pltpu.make_async_remote_copy(
+            src_ref=src,
+            dst_ref=dst,
+            send_sem=sem_s_near.at[n],
+            recv_sem=sem_r_near.at[rnd, back],
+            device_id=(g, y + dy, x + dx),
+            device_id_type=MESH,
+        )
+
+    def near_wait(rnd, n):
+        dy, dx = near[n]
+        if dy == 0:
+            ref = got_col[rnd].at[(dx + 1) // 2]
+        elif dx == 0:
+            ref = got_row[rnd].at[(dy + 1) // 2]
+        else:
+            ref = got_pack[rnd].at[(dy + 1) + (dx + 1) // 2]
+        return pltpu.make_async_remote_copy(
+            src_ref=ref,
+            dst_ref=ref,
+            send_sem=sem_s_near.at[n],
+            recv_sem=sem_r_near.at[rnd, n],
+            device_id=(g, y + dy, x + dx),
+            device_id_type=MESH,
+        )
+
+    def is_me(tg, ty, tx):
+        return (g == tg) & (y == ty) & (x == tx)
+
+    def rim_piece(rnd, kind):
+        if kind == 0:
+            return fields[rnd].at[:, :, at_end[0]]
+        return cols[rnd].at[side[1]]
+
+    def each_rim(kind, visit):
+        for which, off in ((0, 0), (1, 1), (2, -1)):
+            block = last - place[kind] + off
+            fits = live[kind] & (block >= 0) & (block <= last)
+            block = jnp.clip(block, 0, last)
+            for e2 in range(4):
+                ty, tx = tile_place(e2, block, blocks)
+                for g2 in range(groups):
+                    visit(which, e2, g2, (g2, ty, tx), fits)
+
+    def rim_send(rnd, kind):
+        def visit(which, e2, g2, target, ok):
+            mine = is_me(*target)
+            if which == 0:
+                src = rim_piece(rnd, kind)
+                dst = got_rim[rnd][e2 % 2].at[edge[kind], g]
+                send, recv = sem_s_rim.at[kind, e2, g2], sem_r_rim.at[rnd, e2 % 2, edge[kind], g]
+            else:
+                src = packs[rnd].at[head_pack[kind] if which == 1 else tail_pack[kind]]
+                dst = got_end[rnd][e2 % 2].at[which - 1, edge[kind], g]
+                send = sem_s_end.at[kind, which - 1, e2, g2]
+                recv = sem_r_end.at[rnd, e2 % 2, which - 1, edge[kind], g]
+
+            @pl.when(ok & jnp.logical_not(mine))
+            def _():
+                pltpu.make_async_remote_copy(
+                    src_ref=src, dst_ref=dst, send_sem=send, recv_sem=recv, device_id=target, device_id_type=MESH
+                ).start()
+
+            @pl.when(ok & mine)
+            def _():
+                dst[...] = src[...]
+
+        each_rim(kind, visit)
+
+    def rim_wait_send(rnd, kind):
+        def visit(which, e2, g2, target, ok):
+            if which == 0:
+                src = rim_piece(rnd, kind)
+                send, recv = sem_s_rim.at[kind, e2, g2], sem_r_rim.at[rnd, e2 % 2, edge[kind], g]
+            else:
+                src = packs[rnd].at[head_pack[kind] if which == 1 else tail_pack[kind]]
+                send = sem_s_end.at[kind, which - 1, e2, g2]
+                recv = sem_r_end.at[rnd, e2 % 2, which - 1, edge[kind], g]
+
+            @pl.when(ok & jnp.logical_not(is_me(*target)))
+            def _():
+                pltpu.make_async_remote_copy(
+                    src_ref=src, dst_ref=src, send_sem=send, recv_sem=recv, device_id=target, device_id_type=MESH
+                ).wait_send()
+
+        each_rim(kind, visit)
+
+    def rim_wait(rnd, kind):
+        def visit(which, e2, g2, source, ok):
+            if which == 0:
+                ref = got_rim[rnd][kind].at[e2, g2]
+                send, recv = sem_s_rim.at[kind, e2, g2], sem_r_rim.at[rnd, kind, e2, g2]
+            else:
+                ref = got_end[rnd][kind].at[which - 1, e2, g2]
+                send, recv = sem_s_end.at[kind, which - 1, e2, g2], sem_r_end.at[rnd, kind, which - 1, e2, g2]
+
+            @pl.when(ok & jnp.logical_not(is_me(*source)))
+            def _():
+                pltpu.make_async_remote_copy(
+                    src_ref=ref, dst_ref=ref, send_sem=send, recv_sem=recv, device_id=source, device_id_type=MESH
+                ).wait_recv()
+
+        each_rim(kind, visit)
+
+    sub = lax.broadcasted_iota(jnp.int32, (SIDE, 128), 0)
+    lane = lax.broadcasted_iota(jnp.int32, (SIDE, 128), 1)
+    low = lane < HALF
+    node = sub % 4
+    table = deriv_table()
+    weights = (1.0 / 6.0, 5.0 / 6.0, 5.0 / 6.0, 1.0 / 6.0)
+    zero = jnp.zeros((SIDE, 128), jnp.float32)
+
+    def per_node(entries):
+        total = jnp.full((SIDE, 128), entries[0], jnp.float32)
+        for j in range(1, 4):
+            total = jnp.where(node == j, jnp.float32(entries[j]), total)
+        return total
+
+    col_weight = per_node(weights)
+    taps = {
+        s: per_node([float(table[j, j + s]) if 0 <= j + s < 4 else 0.0 for j in range(4)])
+        for s in range(-3, 4)
+    }
+
+    def roll_rows(v, shift):
+        return pltpu.roll(v, (-shift) % SIDE, 0)
+
+    def swap(v):
+        return pltpu.roll(v, HALF, 1)
+
+    def dx(v):
+        total = taps[0] * v
+        for s in (-3, -2, -1, 1, 2, 3):
+            total = total + taps[s] * roll_rows(v, s)
+        return total
+
+    def dy(rows):
+        return [sum(jnp.float32(table[i, k]) * rows[k] for k in range(4)) for i in range(4)]
+
+    def join(v):
+        return v + jnp.where(sub == 3, roll_rows(v, 1), zero) + jnp.where(sub == 4, roll_rows(v, -1), zero)
+
+    def wide(ref, index, r):
+        row = jnp.broadcast_to(ref[index + (pl.ds(r, 1), slice(None))].reshape(1, SIDE), (SIDE, SIDE))
+        eye = lax.broadcasted_iota(jnp.int32, (SIDE, SIDE), 0) == lax.broadcasted_iota(jnp.int32, (SIDE, SIDE), 1)
+        return jnp.broadcast_to(jnp.sum(jnp.where(eye, row, 0.0), axis=1, keepdims=True), (SIDE, 128))
+
+    def store_field(rnd, part, f, above, rows):
+        kept = []
+        for e_row, values in enumerate(rows):
+            kept.append([join(v) for v in values])
+        for e_row in range(len(kept) - 1):
+            both = kept[e_row][3] + kept[e_row + 1][0]
+            kept[e_row][3] = both
+            kept[e_row + 1][0] = both
+        flat = [v for values in kept for v in values]
+        for r, v in enumerate(flat):
+            fields[rnd][part, f, r] = v
+            cols[rnd][0, part, f, pl.ds(r, 1)] = v[0:1]
+            cols[rnd][1, part, f, pl.ds(r, 1)] = v[SIDE - 1 : SIDE]
+        for w in range(4):
+            v = flat[(SIDE - 1) * (w // 2)]
+            c = (SIDE - 1) * (w % 2)
+            packs[rnd][w, pl.ds(part * faces + f, 1)] = v[c : c + 1]
+
+    def exchange(rnd):
+        for n, (dy_, dx_) in enumerate(near):
+
+            @pl.when(has(dy_, dx_))
+            def _():
+                near_copy(rnd, n).start()
+
+        for kind in range(2):
+            rim_send(rnd, kind)
+
+        for n, (dy_, dx_) in enumerate(near):
+            ok = has(dy_, dx_)
+            if dy_ == 0:
+                ref = got_col[rnd].at[(dx_ + 1) // 2]
+            elif dx_ == 0:
+                ref = got_row[rnd].at[(dy_ + 1) // 2]
+            else:
+                ref = got_pack[rnd].at[(dy_ + 1) + (dx_ + 1) // 2]
+
+            @pl.when(ok)
+            def _():
+                near_wait(rnd, n).wait_recv()
+
+            @pl.when(jnp.logical_not(ok))
+            def _():
+                ref[...] = jnp.zeros(ref.shape, jnp.float32)
+
+        for part in range(2):
+            for f in range(faces):
+                for r in range(SIDE):
+                    v = fields[rnd][part, f, r]
+                    west = jnp.broadcast_to(got_col[rnd][0, part, f, pl.ds(r, 1)], (SIDE, 128))
+                    east = jnp.broadcast_to(got_col[rnd][1, part, f, pl.ds(r, 1)], (SIDE, 128))
+                    if r in (0, SIDE - 1):
+                        w = 0 if r == 0 else 1
+                        v = v + got_row[rnd][w, part, f]
+                        west = west + jnp.broadcast_to(got_pack[rnd][2 * w, pl.ds(part * faces + f, 1)], (SIDE, 128))
+                        east = east + jnp.broadcast_to(got_pack[rnd][2 * w + 1, pl.ds(part * faces + f, 1)], (SIDE, 128))
+                    summed[part, f, r] = v + jnp.where(sub == 0, west, jnp.where(sub == SIDE - 1, east, zero))
+
+        for kind in range(2):
+            rim_wait(rnd, kind)
+            has_head = place[kind] > 0
+            has_tail = place[kind] < last
+            first_at = jnp.where(edge[kind] >= 2, SIDE - 1, 0)
+
+            @pl.when(live[kind] & jnp.logical_not(has_head))
+            def _():
+                got_end[rnd][kind][0] = jnp.zeros(got_end[rnd][kind].shape[1:], jnp.float32)
+
+            @pl.when(live[kind] & jnp.logical_not(has_tail))
+            def _():
+                got_end[rnd][kind][1] = jnp.zeros(got_end[rnd][kind].shape[1:], jnp.float32)
+
+            @pl.when(live[kind])
+            def _():
+                for f in range(faces):
+                    nf = nbr_face[g * faces + f, edge[kind]]
+                    ne = nbr_edge[g * faces + f, edge[kind]]
+                    ng, nl = nf // faces, nf % faces
+                    quarter = (edge[kind] - ne + 2) % 4
+                    cosine = jnp.where(quarter == 0, 1.0, jnp.where(quarter == 2, -1.0, 0.0))
+                    sine = jnp.where(quarter == 1, 1.0, jnp.where(quarter == 3, -1.0, 0.0))
+                    sine = jnp.where(low, -sine, sine)
+                    turned = (1 + jnp.where(edge[kind] >= 2, 1, 0) + jnp.where(ne >= 2, 1, 0)) % 2
+                    for part in range(2):
+                        rim = got_rim[rnd][kind][ne, ng, part, nl]
+                        ends = []
+                        for which in range(2):
+                            at = part * faces + nl
+                            ends.append(
+                                jnp.broadcast_to(got_end[rnd][kind][which, ne, ng, pl.ds(at, 1)], (SIDE, 128))
+                            )
+                        b = jnp.where(sub % 2 == 0, roll_rows(rim, 1), roll_rows(rim, -1))
+                        b = jnp.where(sub % 4 < 2, roll_rows(b, 2), roll_rows(b, -2))
+                        b = pltpu.roll(b, 4, 0)
+                        rim = jnp.where(turned == 1, b, rim)
+                        rim = rim + jnp.where(sub == first_at, ends[0], jnp.where(sub == SIDE - 1 - first_at, ends[1], zero))
+                        if part == 0:
+                            rim = cosine * rim + sine * swap(rim)
+                        if kind == 0:
+                            summed[part, f, at_end[0]] += rim
+                        else:
+                            for r in range(SIDE):
+                                summed[part, f, r] += jnp.where(
+                                    sub == at_end[1], jnp.broadcast_to(rim[r : r + 1], (SIDE, 128)), zero
+                                )
+
+        for n, (dy_, dx_) in enumerate(near):
+
+            @pl.when(has(dy_, dx_))
+            def _():
+                near_copy(rnd, n).wait_send()
+
+        for kind in range(2):
+            rim_wait_send(rnd, kind)
+
+    for f in range(faces):
+        a_rows, b_rows = [], []
+        for e_row in range(SIDE // 4):
+            rows = range(4 * e_row, 4 * e_row + 4)
+            wind, temp, contra, energy, vol, cor, mass = [], [], [], [], [], [], []
+            for r in rows:
+                j = wide(jac, (f,), r)
+                m_xx, m_yy, m_xy = wide(diag, (0, f), r), wide(diag, (1, f), r), wide(cross, (f,), r)
+                flux_a[f, r] = j * m_xx
+                flux_b[f, r] = j * m_xy
+                flux_c[f, r] = j * m_yy
+                w = state[f, r, :, 0 : 2 * HALF]
+                t = state[f, r, :, 2 * HALF : 3 * HALF]
+                t = jnp.concatenate([t, t], axis=1)
+                c = jnp.where(low, m_xx, m_yy) * w + m_xy * swap(w)
+                p = w * c
+                wind.append(w)
+                temp.append(t)
+                contra.append(c)
+                energy.append(0.5 * (p + swap(p)) + t)
+                vol.append(j)
+                cor.append(wide(coriolis, (f,), r))
+                mass.append(j * (jnp.float32(weights[r % 4]) * col_weight))
+            dxs = [dx(jnp.where(low, energy[i], wind[i])) for i in range(4)]
+            dys = dy([jnp.where(low, wind[i], energy[i]) for i in range(4)])
+            dxt = [dx(temp[i]) for i in range(4)]
+            dyt = dy(temp)
+            a_out, b_out = [], []
+            for i in range(4):
+                dxv = jnp.where(low, swap(dxs[i]), dxs[i])
+                dyu = jnp.where(low, dys[i], swap(dys[i]))
+                spin = (dxv - dyu) + cor[i] * vol[i]
+                spin = jnp.where(low, spin, -spin)
+                tend = spin * swap(contra[i]) - jnp.where(low, dxs[i], dys[i])
+                a_out.append(mass[i] * (wind[i] + time_step * tend))
+                q = contra[i] * jnp.where(low, dxt[i], dyt[i])
+                b_out.append(mass[i] * jnp.where(low, temp[i] - time_step * (q + swap(q)), 1.0))
+            a_rows.append(a_out)
+            b_rows.append(b_out)
+        store_field(0, 0, f, None, a_rows)
+        store_field(0, 1, f, None, b_rows)
+
+    pl.semaphore_wait(barrier, groups * blocks * blocks - 1)
+    exchange(0)
+
+    def laplacian(rnd, source):
+        for f in range(faces):
+            for part in range(2):
+                out_rows = []
+                for e_row in range(SIDE // 4):
+                    rows = range(4 * e_row, 4 * e_row + 4)
+                    values = [source(part, f, r) for r in rows]
+                    gx = [dx(v) for v in values]
+                    gy = dy(values)
+                    fx = [flux_a[f, r] * gx[i] + flux_b[f, r] * gy[i] for i, r in enumerate(rows)]
+                    fy = [flux_b[f, r] * gx[i] + flux_c[f, r] * gy[i] for i, r in enumerate(rows)]
+                    fyy = dy(fy)
+                    out_rows.append(
+                        [(jnp.float32(weights[i]) * col_weight) * (dx(fx[i]) + fyy[i]) for i in range(4)]
+                    )
+                store_field(rnd, part, f, None, out_rows)
+
+    for f in range(faces):
+        for r in range(SIDE):
+            b = summed[1, f, r]
+            inv = 1.0 / jnp.where(low, swap(b), b)
+            inverse[f, r] = inv
+            out[f, r, :, 0 : 2 * HALF] = summed[0, f, r] * inv
+            out[f, r, :, 2 * HALF : 3 * HALF] = (b * inv)[:, 0:HALF]
+            summed[0, f, r] = summed[0, f, r] * inv
+            summed[1, f, r] = b * inv
+    laplacian(1, lambda part, f, r: summed[part, f, r])
+    exchange(1)
+    laplacian(2, lambda part, f, r: summed[part, f, r] * inverse[f, r])
+    exchange(2)
+    for f in range(faces):
+        for r in range(SIDE):
+            scale = hyper_coeff * inverse[f, r]
+            out[f, r, :, 0 : 2 * HALF] = out[f, r, :, 0 : 2 * HALF] - scale * summed[0, f, r]
+            out[f, r, :, 2 * HALF : 3 * HALF] = (
+                out[f, r, :, 2 * HALF : 3 * HALF] - (scale * summed[1, f, r])[:, 0:HALF]
+            )
+
+
+def fused(groups, blocks, state, jacobian, metric_diag, metric_cross, coriolis, nbr_face, nbr_edge):
+    faces = state.shape[0]
+    piece = (2, faces, SIDE, 128)
+    tile = (faces, SIDE, SIDE, 128)
+
+    def per_round(shape):
+        return [pltpu.VMEM(shape, jnp.float32)] * ROUNDS
+
+    scratch = (
+        per_round((2,) + tile)
+        + per_round((2,) + piece)
+        + per_round((4, SIDE, 128))
+        + per_round((2,) + piece)
+        + per_round((2,) + piece)
+        + per_round((4, SIDE, 128))
+        + per_round((4, groups) + piece) * 2
+        + per_round((2, 4, groups, SIDE, 128)) * 2
+        + [pltpu.VMEM((2,) + tile, jnp.float32)]
+        + [pltpu.VMEM(tile, jnp.float32)] * 4
+        + [
+            pltpu.SemaphoreType.DMA((8,)),
+            pltpu.SemaphoreType.DMA((ROUNDS, 8)),
+            pltpu.SemaphoreType.DMA((2, 4, groups)),
+            pltpu.SemaphoreType.DMA((ROUNDS, 2, 4, groups)),
+            pltpu.SemaphoreType.DMA((2, 2, 4, groups)),
+            pltpu.SemaphoreType.DMA((ROUNDS, 2, 2, 4, groups)),
+        ]
+    )
+    vmem, smem = pl.BlockSpec(memory_space=pltpu.VMEM), pl.BlockSpec(memory_space=pltpu.SMEM)
+    return pl.pallas_call(
+        functools.partial(kernel, groups, blocks),
+        out_shape=jax.ShapeDtypeStruct(state.shape, jnp.float32),
+        in_specs=[smem, smem] + [vmem] * 5,
+        out_specs=vmem,
+        scratch_shapes=scratch,
+        compiler_params=pltpu.CompilerParams(collective_id=0, has_side_effects=True),
+    )(nbr_face, nbr_edge, state, jacobian, metric_diag, metric_cross, coriolis)
+
+
 def solution(mesh):
+    groups, rows, columns = (mesh.shape[axis] for axis in ("face", "fy", "fx"))
+
+    def body(*args):
+        state = args[0]
+        faces = state.shape[0]
+        if rows == columns and rows > 1 and state.shape[1:] == (SIDE, SIDE, 3 * HALF) and 2 * faces <= SIDE:
+            return fused(groups, rows, *args)
+        return per_device(*args)
+
     return jax.shard_map(
-        per_device,
+        body,
         mesh=mesh,
         in_specs=(
             P("face", "fy", "fx", None),

time: 373 us -> 42.2 us (0.11)
  waiting for transfers between devices: 139 us -> 0 us
  blocking collectives: 99.7 us -> 0 us
  starting transfers between devices: 69.1 us -> 0 us
  Pallas kernels: 0 us -> 38.4 us
  local copies, waits for them, and re-layouts: 26.4 us -> 3.66 us
  between operations: 16.4 us -> 0.01 us
  other arithmetic: 12.6 us -> 0 us
  matrix products: 7.16 us -> 0 us
    unnamed x9 -> x0, waiting for transfers between devices: 103 us -> none
    psum x6 -> x0, blocking collectives: 86.5 us -> none  [the longest x3 54.8 us: assemble(): tall_whole = lax.psum(tall_lines, 'fx')]
    ppermute x16 -> x0, starting transfers between devices: 41.9 us -> none  [the longest x8 31.5 us: padded(): lax.ppermute(tail, axis, [(i, (i + 1) % count) for i in range(ends)])]
    pallas_call x0 -> x1, Pallas kernels: none -> 38.4 us  [fused(): pl.pallas_call(functools.partial(kernel, groups, blocks), out_shape=jax.S...]
    all_to_all x8 -> x0, waiting for transfers between devices: 31.1 us -> none  [the longest x4 16.2 us: assemble(): lax.all_to_all(send_tall, 'face', split_axis=0, concat_axis=1, tiled=True)]
    all_to_all x8 -> x0, starting transfers between devices: 27 us -> none  [the longest x4 13.5 us: assemble(): lax.all_to_all(send_flat, 'face', split_axis=0, concat_axis=1, tiled=True)]
    unnamed x1 -> x0, blocking collectives: 13.3 us -> none
    dot_general x18 -> x0, matrix products: 7.16 us -> none  [the longest x5 2.75 us: along_y(): jnp.einsum('ik,aekxc->aeixc', jnp.asarray(deriv_table(), jnp.float32), bl...]
  transfers between devices with their start and end apart: 30 -> 0, of which waited for: 16 -> 0; matrix products, arithmetic and copies ran while one was open for 5% -> 0% of each run, Pallas kernels for 0% -> 0%
where the time goes in v1:
time: 42.2 us; the launch traced here: 42 us
  Pallas kernels  38.4 us (91%)
  local copies, waits for them, and re-layouts  3.66 us (9%)
    pallas_call x1, Pallas kernels, fused(): pl.pallas_call(functools.partial(kernel, groups, blocks), out_shape=jax.S...  38.4 us
    unnamed x5, local copies, waits for them, and re-layouts  3.66 us

profile of v1, /device:TPU:0, one launch (start us, length us, event | category | flops | bytes accessed | tf_op | source)
XLA Modules:
  0.0 42.0 jit_solution(15527987363914612621)
XLA Ops:
  0.0 0.0 copy-start
  0.0 1.4 %copy.8.nbr_face = s32[6,4]{1,0:T(8,128)} copy(s32[6,4]{0,1:T(4,128)} %param.12) | data formatting | bytes 192 | tf_op args[5]
  1.4 0.0 copy-done
  1.4 0.7 %copy.9.nbr_edge = s32[6,4]{1,0:T(8,128)} copy(s32[6,4]{0,1:T(4,128)S(1)} %copy-done) | data formatting | bytes 192 | tf_op args[6]
  2.0 38.4 %shard_map.73 = f32[3,8,8,192]{3,2,1,0:T(8,128)} custom-call(s32[6,4]{1,0:T(8,128)} %copy.8.nbr_face, s32[6,4]{1,0:T(8,128)} %copy.9.nbr_edge, f32[3,8,8,192]{3,2,1,0:T(8,128)} %state.1, f32[3,8,8]{2,1,0:T(8,128)} %jac.1, f32[2,3,8,8]{3,2,1,0:T(8,128)} %diag.1, f32[3,8,8]{2,1,0:T(8,128)} %cross.1, f32[3,8,8]{2,1,0:T(8,128)} %coriolis.1), custom_call_target="tpu_custom_call" | custom-call | tf_op jit(solution)/shard_map/pallas_call | solution.py:730
  40.4 1.6 %copy.11 = f32[3,8,8,192]{3,2,1,0:T(8,128)} copy(f32[3,8,8,192]{3,2,1,0:T(8,128)} %shard_map.73) | data formatting | bytes 294912
Async XLA Ops:
  0.0 1.4 %copy-start = (s32[6,4]{0,1:T(4,128)S(1)}, s32[6,4]{0,1:T(4,128)}, u32[]{:S(2)}) copy-start(s32[6,4]{0,1:T(4,128)} %param.13) | copy-start | bytes 292

commit v2 on v0

--- a/solution.py
+++ b/solution.py
@@ -1,11 +1,17 @@
+import functools
+
 import jax
 import jax.numpy as jnp
 import numpy as np
 from jax import lax
+from jax.experimental import pallas as pl
+from jax.experimental.pallas import tpu as pltpu
 from jax.sharding import PartitionSpec as P
 
 time_step = 0.05
 hyper_coeff = 0.0005
+MESH = pl.DeviceIdType.MESH
+ROUNDS = 3
 
 
 def padded(cells, sides, width):
@@ -267,9 +273,512 @@
     return sectioned - hyper_coeff * second_lap
 
 
+SIDE = 8
+HALF = 64
+
+
+def tile_place(edge, kind, block, last):
+    if kind == 0:
+        return jnp.where(edge == 0, 0, last), jnp.where(edge == 0, block, last - block)
+    return jnp.where(edge == 1, block, last - block), jnp.where(edge == 1, last, 0)
+
+
+def kernel(
+    groups,
+    blocks,
+    nbr_face,
+    nbr_edge,
+    state,
+    jac,
+    diag,
+    cross,
+    coriolis,
+    out,
+    *scratch,
+):
+    faces = state.shape[0]
+    pairs = (faces + 1) // 2
+    planes = faces + pairs
+    fields, cols, packs, got_col, got_row, got_pack, rim_0, rim_1, end_0, end_1 = (
+        scratch[i * ROUNDS : (i + 1) * ROUNDS] for i in range(10)
+    )
+    got_rim = [pair for pair in zip(rim_0, rim_1)]
+    got_end = [pair for pair in zip(end_0, end_1)]
+    summed, sectioned, inverse, flux_a, flux_b, flux_c = scratch[10 * ROUNDS : 10 * ROUNDS + 6]
+    sem_s_near, sem_r_near, sem_s_rim, sem_r_rim, sem_s_end, sem_r_end = scratch[10 * ROUNDS + 6 :]
+    g = lax.axis_index("face")
+    y = lax.axis_index("fy")
+    x = lax.axis_index("fx")
+    last = blocks - 1
+
+    barrier = pltpu.get_barrier_semaphore()
+    for tg in range(groups):
+        for ty in range(blocks):
+            for tx in range(blocks):
+
+                @pl.when(jnp.logical_not((g == tg) & (y == ty) & (x == tx)))
+                def _():
+                    pl.semaphore_signal(barrier, inc=1, device_id=(tg, ty, tx), device_id_type=MESH)
+
+    live = ((y == 0) | (y == last), (x == 0) | (x == last))
+    edge = (jnp.where(y == 0, 0, 2), jnp.where(x == 0, 3, 1))
+    place = (jnp.where(y == 0, x, last - x), jnp.where(x == 0, last - y, y))
+    at_end = (jnp.where(y == 0, 0, SIDE - 1), jnp.where(x == 0, 0, SIDE - 1))
+    side = (jnp.where(y == 0, 0, 1), jnp.where(x == 0, 0, 1))
+    head_pack = (jnp.where(y == 0, 0, 3), jnp.where(x == 0, 2, 1))
+    tail_pack = (jnp.where(y == 0, 1, 2), jnp.where(x == 0, 0, 3))
+
+    near = [(0, -1), (0, 1), (-1, 0), (1, 0), (-1, -1), (-1, 1), (1, -1), (1, 1)]
+
+    def has(dy, dx):
+        ok = None
+        for d, at in ((dy, y), (dx, x)):
+            if d:
+                one = at > 0 if d < 0 else at < last
+                ok = one if ok is None else ok & one
+        return ok
+
+    def near_slot(rnd, n):
+        dy, dx = near[n]
+        if dy == 0:
+            return got_col[rnd].at[(dx + 1) // 2]
+        if dx == 0:
+            return got_row[rnd].at[(dy + 1) // 2]
+        return got_pack[rnd].at[(dy + 1) + (dx + 1) // 2]
+
+    def near_copy(rnd, n):
+        dy, dx = near[n]
+        back = near.index((-dy, -dx))
+        if dy == 0:
+            src = cols[rnd].at[(dx + 1) // 2]
+        elif dx == 0:
+            src = fields[rnd].at[:, (dy + 1) // 2 * (SIDE - 1)]
+        else:
+            src = packs[rnd].at[(dy + 1) + (dx + 1) // 2]
+        return pltpu.make_async_remote_copy(
+            src_ref=src,
+            dst_ref=near_slot(rnd, back),
+            send_sem=sem_s_near.at[n],
+            recv_sem=sem_r_near.at[rnd, back],
+            device_id=(g, y + dy, x + dx),
+            device_id_type=MESH,
+        )
+
+    def near_wait(rnd, n):
+        dy, dx = near[n]
+        pltpu.make_async_remote_copy(
+            src_ref=near_slot(rnd, n),
+            dst_ref=near_slot(rnd, n),
+            send_sem=sem_s_near.at[n],
+            recv_sem=sem_r_near.at[rnd, n],
+            device_id=(g, y + dy, x + dx),
+            device_id_type=MESH,
+        ).wait_recv()
+
+    def each_rim(kind, which, visit):
+        block = last - place[kind] + (0, 1, -1)[which]
+
+        @pl.when(live[kind] & (block >= 0) & (block <= last))
+        def _():
+            for de in range(4):
+                e2, kind2 = lax.rem(edge[kind] + de, 4), (kind + de) % 2
+                ty, tx = tile_place(e2, kind2, block, last)
+                for dg in range(groups):
+                    g2 = lax.rem(g + dg, groups)
+                    own = dg == 0 and (de in (1, 3) if which == 0 else de == 0)
+                    visit(de, dg, e2, kind2, g2, (g2, ty, tx), (y == ty) & (x == tx) if own else None)
+
+    def sides(mine, here, there):
+        if mine is None:
+            there()
+            return
+        pl.when(jnp.logical_not(mine))(there)
+        if here is not None:
+            pl.when(mine)(here)
+
+    def rim_source(rnd, kind, which):
+        if which == 0:
+            return fields[rnd].at[:, at_end[0]] if kind == 0 else cols[rnd].at[side[1]]
+        return packs[rnd].at[head_pack[kind] if which == 1 else tail_pack[kind]]
+
+    def rim_slot(rnd, kind, which, e2, g2):
+        if which == 0:
+            return got_rim[rnd][kind].at[e2, g2], sem_r_rim.at[rnd, kind, e2, g2]
+        return got_end[rnd][kind].at[which - 1, e2, g2], sem_r_end.at[rnd, kind, which - 1, e2, g2]
+
+    def rim_sent(kind, which, de, dg):
+        return sem_s_rim.at[kind, de, dg] if which == 0 else sem_s_end.at[kind, which - 1, de, dg]
+
+    def rim_send(rnd, kind, which):
+        src = rim_source(rnd, kind, which)
+
+        def visit(de, dg, e2, kind2, g2, target, mine):
+            dst, recv = rim_slot(rnd, kind2, which, edge[kind], g)
+
+            def there():
+                pltpu.make_async_remote_copy(
+                    src_ref=src,
+                    dst_ref=dst,
+                    send_sem=rim_sent(kind, which, de, dg),
+                    recv_sem=recv,
+                    device_id=target,
+                    device_id_type=MESH,
+                ).start()
+
+            def here():
+                dst[...] = src[...]
+
+            sides(mine, here, there)
+
+        each_rim(kind, which, visit)
+
+    def rim_wait_send(rnd, kind, which):
+        src = rim_source(rnd, kind, which)
+
+        def visit(de, dg, e2, kind2, g2, target, mine):
+            dst, recv = rim_slot(rnd, kind2, which, edge[kind], g)
+
+            def there():
+                pltpu.make_async_remote_copy(
+                    src_ref=src,
+                    dst_ref=dst,
+                    send_sem=rim_sent(kind, which, de, dg),
+                    recv_sem=recv,
+                    device_id=target,
+                    device_id_type=MESH,
+                ).wait_send()
+
+            sides(mine, None, there)
+
+        each_rim(kind, which, visit)
+
+    def rim_wait(rnd, kind, which):
+        def visit(de, dg, e2, kind2, g2, source, mine):
+            dst, recv = rim_slot(rnd, kind, which, e2, g2)
+
+            def there():
+                pltpu.make_async_remote_copy(
+                    src_ref=dst,
+                    dst_ref=dst,
+                    send_sem=rim_sent(kind, which, de, dg),
+                    recv_sem=recv,
+                    device_id=source,
+                    device_id_type=MESH,
+                ).wait_recv()
+
+            sides(mine, None, there)
+
+        each_rim(kind, which, visit)
+
+    sub = lax.broadcasted_iota(jnp.int32, (SIDE, 128), 0)
+    lane = lax.broadcasted_iota(jnp.int32, (SIDE, 128), 1)
+    low = lane < HALF
+    node = sub % 4
+    table = deriv_table()
+    weights = (1.0 / 6.0, 5.0 / 6.0, 5.0 / 6.0, 1.0 / 6.0)
+    zero = jnp.zeros((SIDE, 128), jnp.float32)
+
+    def per_node(entries):
+        total = jnp.full((SIDE, 128), entries[0], jnp.float32)
+        for j in range(1, 4):
+            total = jnp.where(node == j, jnp.float32(entries[j]), total)
+        return total
+
+    col_weight = per_node(weights)
+    taps = {
+        s: per_node([float(table[j, j + s]) if 0 <= j + s < 4 else 0.0 for j in range(4)])
+        for s in range(-3, 4)
+    }
+
+    def roll_rows(v, shift):
+        return pltpu.roll(v, (-shift) % SIDE, 0)
+
+    def swap(v):
+        return pltpu.roll(v, HALF, 1)
+
+    def dx(v):
+        total = taps[0] * v
+        for s in (-3, -2, -1, 1, 2, 3):
+            total = total + taps[s] * roll_rows(v, s)
+        return total
+
+    def dy(rows):
+        return [sum(jnp.float32(table[i, k]) * rows[k] for k in range(4)) for i in range(4)]
+
+    def join(v):
+        return v + jnp.where(sub == 3, roll_rows(v, 1), jnp.where(sub == 4, roll_rows(v, -1), zero))
+
+    def wide(ref, index, r):
+        row = jnp.broadcast_to(ref[index + (pl.ds(r, 1), slice(None))].reshape(1, SIDE), (SIDE, SIDE))
+        eye = lax.broadcasted_iota(jnp.int32, (SIDE, SIDE), 0) == lax.broadcasted_iota(jnp.int32, (SIDE, SIDE), 1)
+        return jnp.broadcast_to(jnp.sum(jnp.where(eye, row, 0.0), axis=1, keepdims=True), (SIDE, 128))
+
+    def mass_mix(values):
+        total = values[0]
+        for f in range(1, faces):
+            total = jnp.where(lane >= HALF + 16 * f, values[f], total)
+        return total
+
+    def pair_up(values, spare):
+        return [
+            jnp.where(low, values[2 * i], values[2 * i + 1] if 2 * i + 1 < faces else spare)
+            for i in range(pairs)
+        ]
+
+    def store_field(rnd, plane, rows):
+        rows = [join(v) for v in rows]
+        for r in range(4, SIDE, 4):
+            both = rows[r - 1] + rows[r]
+            rows[r - 1] = both
+            rows[r] = both
+        for r, v in enumerate(rows):
+            fields[rnd][plane, r] = v
+            cols[rnd][0, plane, pl.ds(r, 1)] = v[0:1]
+            cols[rnd][1, plane, pl.ds(r, 1)] = v[SIDE - 1 : SIDE]
+        for w in range(4):
+            v = rows[(SIDE - 1) * (w // 2)]
+            c = (SIDE - 1) * (w % 2)
+            packs[rnd][w, pl.ds(plane, 1)] = v[c : c + 1]
+
+    def mirror(v):
+        v = jnp.where(sub % 2 == 0, roll_rows(v, 1), roll_rows(v, -1))
+        v = jnp.where(sub % 4 < 2, roll_rows(v, 2), roll_rows(v, -2))
+        return pltpu.roll(v, 4, 0)
+
+    def exchange(rnd):
+        for n, (dy_, dx_) in enumerate(near):
+            pl.when(has(dy_, dx_))(lambda n=n: near_copy(rnd, n).start())
+        for which in range(3):
+            for kind in range(2):
+                rim_send(rnd, kind, which)
+
+        for n, (dy_, dx_) in enumerate(near):
+            ok = has(dy_, dx_)
+            ref = near_slot(rnd, n)
+            pl.when(ok)(lambda n=n: near_wait(rnd, n))
+
+            @pl.when(jnp.logical_not(ok))
+            def _():
+                ref[...] = jnp.zeros(ref.shape, jnp.float32)
+
+        def wide_row(ref, *index):
+            return jnp.broadcast_to(ref[index], (SIDE, 128))
+
+        for plane in range(planes):
+            for r in range(SIDE):
+                v = fields[rnd][plane, r]
+                west = wide_row(got_col[rnd], 0, plane, pl.ds(r, 1))
+                east = wide_row(got_col[rnd], 1, plane, pl.ds(r, 1))
+                if r in (0, SIDE - 1):
+                    w = 0 if r == 0 else 1
+                    v = v + got_row[rnd][w, plane]
+                    west = west + wide_row(got_pack[rnd], 2 * w, pl.ds(plane, 1))
+                    east = east + wide_row(got_pack[rnd], 2 * w + 1, pl.ds(plane, 1))
+                summed[plane, r] = v + jnp.where(sub == 0, west, jnp.where(sub == SIDE - 1, east, zero))
+
+        for kind in range(2):
+            for which in range(3):
+                rim_wait(rnd, kind, which)
+
+            @pl.when(live[kind] & (place[kind] == 0))
+            def _():
+                got_end[rnd][kind][0] = jnp.zeros(got_end[rnd][kind].shape[1:], jnp.float32)
+
+            @pl.when(live[kind] & (place[kind] == last))
+            def _():
+                got_end[rnd][kind][1] = jnp.zeros(got_end[rnd][kind].shape[1:], jnp.float32)
+
+            @pl.when(live[kind])
+            def _():
+                first_at = jnp.where(edge[kind] >= 2, SIDE - 1, 0)
+                winds, temps, masses = [], [], []
+                for f in range(faces):
+                    nf = nbr_face[edge[kind], g * faces + f]
+                    ne = nbr_edge[edge[kind], g * faces + f]
+                    ng, nl = nf // faces, nf % faces
+                    quarter = (edge[kind] - ne + 2) % 4
+                    cosine = jnp.where(quarter == 0, 1.0, jnp.where(quarter == 2, -1.0, 0.0))
+                    sine = jnp.where(quarter == 1, 1.0, jnp.where(quarter == 3, -1.0, 0.0))
+                    sine = jnp.where(low, -sine, sine)
+                    turned = (1 + jnp.where(edge[kind] >= 2, 1, 0) + jnp.where(ne >= 2, 1, 0)) % 2
+
+                    def partner(plane):
+                        v = got_rim[rnd][kind][ne, ng, plane]
+                        v = jnp.where(turned == 1, mirror(v), v)
+                        head = wide_row(got_end[rnd][kind], 0, ne, ng, pl.ds(plane, 1))
+                        tail = wide_row(got_end[rnd][kind], 1, ne, ng, pl.ds(plane, 1))
+                        return v + jnp.where(
+                            sub == first_at, head, jnp.where(sub == SIDE - 1 - first_at, tail, zero)
+                        )
+
+                    v = partner(nl)
+                    winds.append(cosine * v + sine * swap(v))
+                    v = partner(faces + nl // 2)
+                    temps.append(jnp.where(nl % 2 == f % 2, v, swap(v)))
+                    if rnd == 0:
+                        v = partner(planes - 1)
+                        own = v
+                        for k in range(faces):
+                            if k != f:
+                                own = jnp.where(nl == k, pltpu.roll(v, 16 * (f - k) % 128, 1), own)
+                        masses.append(own)
+                adds = winds + pair_up(temps, mass_mix(masses) if rnd == 0 else zero)
+                for plane, rim in enumerate(adds):
+                    if kind == 0:
+                        summed[plane, at_end[0]] += rim
+                    else:
+                        for r in range(SIDE):
+                            summed[plane, r] += jnp.where(
+                                sub == at_end[1], jnp.broadcast_to(rim[r : r + 1], (SIDE, 128)), zero
+                            )
+
+        for n, (dy_, dx_) in enumerate(near):
+            pl.when(has(dy_, dx_))(lambda n=n: near_copy(rnd, n).wait_send())
+        for which in range(3):
+            for kind in range(2):
+                rim_wait_send(rnd, kind, which)
+
+    section = [[None] * SIDE for _ in range(faces)]
+    heat = [[None] * SIDE for _ in range(faces)]
+    weight = [[None] * SIDE for _ in range(faces)]
+    for f in range(faces):
+        for start in range(0, SIDE, 4):
+            wind, temp, contra, energy, vol, cor = [], [], [], [], [], []
+            for r in range(start, start + 4):
+                j = wide(jac, (f,), r)
+                m_xx, m_yy, m_xy = wide(diag, (0, f), r), wide(diag, (1, f), r), wide(cross, (f,), r)
+                flux_a[f, r] = j * m_xx
+                flux_b[f, r] = j * m_xy
+                flux_c[f, r] = j * m_yy
+                w = state[f, r, :, 0 : 2 * HALF]
+                t = state[f, r, :, 2 * HALF : 3 * HALF]
+                t = jnp.concatenate([t, t], axis=1)
+                c = jnp.where(low, m_xx, m_yy) * w + m_xy * swap(w)
+                p = w * c
+                wind.append(w)
+                temp.append(t)
+                contra.append(c)
+                energy.append(0.5 * (p + swap(p)) + t)
+                vol.append(j)
+                cor.append(wide(coriolis, (f,), r))
+                weight[f][r] = j * (jnp.float32(weights[r % 4]) * col_weight)
+            dxs = [dx(jnp.where(low, energy[i], wind[i])) for i in range(4)]
+            dys = dy([jnp.where(low, wind[i], energy[i]) for i in range(4)])
+            dxt = [dx(temp[i]) for i in range(4)]
+            dyt = dy(temp)
+            for i in range(4):
+                r = start + i
+                dxv = jnp.where(low, swap(dxs[i]), dxs[i])
+                dyu = jnp.where(low, dys[i], swap(dys[i]))
+                spin = (dxv - dyu) + cor[i] * vol[i]
+                spin = jnp.where(low, spin, -spin)
+                tend = spin * swap(contra[i]) - jnp.where(low, dxs[i], dys[i])
+                section[f][r] = weight[f][r] * (wind[i] + time_step * tend)
+                q = contra[i] * jnp.where(low, dxt[i], dyt[i])
+                heat[f][r] = weight[f][r] * (temp[i] - time_step * (q + swap(q)))
+        store_field(0, f, section[f])
+    mixed = [
+        pair_up([heat[f][r] for f in range(faces)], mass_mix([weight[f][r] for f in range(faces)]))
+        for r in range(SIDE)
+    ]
+    for i in range(pairs):
+        store_field(0, faces + i, [mixed[r][i] for r in range(SIDE)])
+
+    pl.semaphore_wait(barrier, groups * blocks * blocks - 1)
+    exchange(0)
+
+    def laplacian(rnd, source):
+        for plane in range(planes):
+            rows = []
+            for start in range(0, SIDE, 4):
+                at = range(start, start + 4)
+                values = [source(plane, r) for r in at]
+                coefs = [[ref[plane, r] for ref in (flux_a, flux_b, flux_c)] for r in at]
+                gx = [dx(v) for v in values]
+                gy = dy(values)
+                fx = [c[0] * p + c[1] * q for c, p, q in zip(coefs, gx, gy)]
+                fy = dy([c[1] * p + c[2] * q for c, p, q in zip(coefs, gx, gy)])
+                rows += [(jnp.float32(weights[i]) * col_weight) * (dx(fx[i]) + fy[i]) for i in range(4)]
+            store_field(rnd, plane, rows)
+
+    for r in range(SIDE):
+        spare = summed[planes - 1, r]
+        inv = []
+        for f in range(faces):
+            at = HALF + 16 * f
+            inv.append(1.0 / jnp.broadcast_to(spare[:, at : at + 1], (SIDE, 128)))
+        for plane, v in enumerate(inv + pair_up(inv, inv[-1])):
+            inverse[plane, r] = v
+            sectioned[plane, r] = summed[plane, r] * v
+        for ref in (flux_a, flux_b, flux_c):
+            mine = [ref[f, r] for f in range(faces)]
+            for i, v in enumerate(pair_up(mine, mine[-1])):
+                ref[faces + i, r] = v
+    laplacian(1, lambda plane, r: sectioned[plane, r])
+    exchange(1)
+    laplacian(2, lambda plane, r: summed[plane, r] * inverse[plane, r])
+    exchange(2)
+    for r in range(SIDE):
+        done = [
+            sectioned[plane, r] - hyper_coeff * (summed[plane, r] * inverse[plane, r]) for plane in range(planes)
+        ]
+        for f in range(faces):
+            out[f, r, :, 0 : 2 * HALF] = done[f]
+            t = done[faces + f // 2]
+            out[f, r, :, 2 * HALF : 3 * HALF] = (t if f % 2 == 0 else swap(t))[:, 0:HALF]
+
+
+def fused(groups, blocks, state, jacobian, metric_diag, metric_cross, coriolis, nbr_face, nbr_edge):
+    faces = state.shape[0]
+    planes = faces + (faces + 1) // 2
+    piece = (planes, SIDE, 128)
+    tile = (planes, SIDE, SIDE, 128)
+
+    def per_round(shape):
+        return [pltpu.VMEM(shape, jnp.float32)] * ROUNDS
+
+    scratch = (
+        per_round(tile)
+        + per_round((2,) + piece)
+        + per_round((4, planes, 128))
+        + per_round((2,) + piece)
+        + per_round((2,) + piece)
+        + per_round((4, planes, 128))
+        + per_round((4, groups) + piece) * 2
+        + per_round((2, 4, groups, planes, 128)) * 2
+        + [pltpu.VMEM(tile, jnp.float32)] * 6
+        + [
+            pltpu.SemaphoreType.DMA((8,)),
+            pltpu.SemaphoreType.DMA((ROUNDS, 8)),
+            pltpu.SemaphoreType.DMA((2, 4, groups)),
+            pltpu.SemaphoreType.DMA((ROUNDS, 2, 4, groups)),
+            pltpu.SemaphoreType.DMA((2, 2, 4, groups)),
+            pltpu.SemaphoreType.DMA((ROUNDS, 2, 2, 4, groups)),
+        ]
+    )
+    vmem, smem = pl.BlockSpec(memory_space=pltpu.VMEM), pl.BlockSpec(memory_space=pltpu.SMEM)
+    return pl.pallas_call(
+        functools.partial(kernel, groups, blocks),
+        out_shape=jax.ShapeDtypeStruct(state.shape, jnp.float32),
+        in_specs=[smem, smem] + [vmem] * 5,
+        out_specs=vmem,
+        scratch_shapes=scratch,
+        compiler_params=pltpu.CompilerParams(collective_id=0, has_side_effects=True),
+    )(nbr_face.T, nbr_edge.T, state, jacobian, metric_diag, metric_cross, coriolis)
+
+
 def solution(mesh):
+    groups, rows, columns = (mesh.shape[axis] for axis in ("face", "fy", "fx"))
+
+    def body(*args):
+        state = args[0]
+        faces = state.shape[0]
+        if rows == columns and rows > 1 and state.shape[1:] == (SIDE, SIDE, 3 * HALF) and faces in (1, 3):
+            return fused(groups, rows, *args)
+        return per_device(*args)
+
     return jax.shard_map(
-        per_device,
+        body,
         mesh=mesh,
         in_specs=(
             P("face", "fy", "fx", None),

time: 373 us -> 37.3 us (0.10)
  waiting for transfers between devices: 139 us -> 0 us
  blocking collectives: 99.7 us -> 0 us
  starting transfers between devices: 69.1 us -> 0 us
  Pallas kernels: 0 us -> 35.5 us
  local copies, waits for them, and re-layouts: 26.4 us -> 1.62 us
  between operations: 16.4 us -> 0.01 us
  other arithmetic: 12.6 us -> 0 us
  matrix products: 7.16 us -> 0 us
    unnamed x9 -> x0, waiting for transfers between devices: 103 us -> none
    psum x6 -> x0, blocking collectives: 86.5 us -> none  [the longest x3 54.8 us: assemble(): tall_whole = lax.psum(tall_lines, 'fx')]
    ppermute x16 -> x0, starting transfers between devices: 41.9 us -> none  [the longest x8 31.5 us: padded(): lax.ppermute(tail, axis, [(i, (i + 1) % count) for i in range(ends)])]
    pallas_call x0 -> x1, Pallas kernels: none -> 35.5 us  [fused(): pl.pallas_call(functools.partial(kernel, groups, blocks), out_shape=jax.S...]
    all_to_all x8 -> x0, waiting for transfers between devices: 31.1 us -> none  [the longest x4 16.2 us: assemble(): lax.all_to_all(send_tall, 'face', split_axis=0, concat_axis=1, tiled=True)]
    all_to_all x8 -> x0, starting transfers between devices: 27 us -> none  [the longest x4 13.5 us: assemble(): lax.all_to_all(send_flat, 'face', split_axis=0, concat_axis=1, tiled=True)]
    unnamed x1 -> x0, blocking collectives: 13.3 us -> none
    unnamed x33 -> x1, local copies, waits for them, and re-layouts: 10.3 us -> 1.62 us
  transfers between devices with their start and end apart: 30 -> 0, of which waited for: 16 -> 0; matrix products, arithmetic and copies ran while one was open for 5% -> 0% of each run, Pallas kernels for 0% -> 0%
where the time goes in v2:
time: 37.3 us; the launch traced here: 37.1 us
  Pallas kernels  35.5 us (95%)
  local copies, waits for them, and re-layouts  1.62 us (4%)
    pallas_call x1, Pallas kernels, fused(): pl.pallas_call(functools.partial(kernel, groups, blocks), out_shape=jax.S...  35.5 us
    unnamed x1, local copies, waits for them, and re-layouts  1.62 us

profile of v2, /device:TPU:0, one launch (start us, length us, event | category | flops | bytes accessed | tf_op | source)
XLA Modules:
  0.0 37.1 jit_solution(14128217666477886957)
XLA Ops:
  0.0 35.5 %shard_map.73 = f32[3,8,8,192]{3,2,1,0:T(8,128)} custom-call(s32[4,6]{1,0:T(4,128)} %bitcast.2, s32[4,6]{1,0:T(4,128)} %bitcast.3, f32[3,8,8,192]{3,2,1,0:T(8,128)} %state.1, f32[3,8,8]{2,1,0:T(8,128)} %jac.1, f32[2,3,8,8]{3,2,1,0:T(8,128)} %diag.1, f32[3,8,8]{2,1,0:T(8,128)} %cross.1, f32[3,8,8]{2,1,0:T(8,128)} %coriolis.1), custom_call_target="tpu_custom_call" | custom-call | tf_op jit(solution)/shard_map/pallas_call | solution.py:760
  35.5 1.6 %copy.9 = f32[3,8,8,192]{3,2,1,0:T(8,128)} copy(f32[3,8,8,192]{3,2,1,0:T(8,128)} %shard_map.73) | data formatting | bytes 294912

commit v3 on v2

--- a/solution.py
+++ b/solution.py
@@ -305,7 +305,7 @@
     got_rim = [pair for pair in zip(rim_0, rim_1)]
     got_end = [pair for pair in zip(end_0, end_1)]
     summed, sectioned, inverse, flux_a, flux_b, flux_c = scratch[10 * ROUNDS : 10 * ROUNDS + 6]
-    sem_s_near, sem_r_near, sem_s_rim, sem_r_rim, sem_s_end, sem_r_end = scratch[10 * ROUNDS + 6 :]
+    sem_s_near, sem_r_near, sem_s_rim, sem_r_rim, sem_s_own, sem_r_own = scratch[10 * ROUNDS + 6 :]
     g = lax.axis_index("face")
     y = lax.axis_index("fy")
     x = lax.axis_index("fx")
@@ -380,7 +380,7 @@
 
         @pl.when(live[kind] & (block >= 0) & (block <= last))
         def _():
-            for de in range(4):
+            for de in (2, 1, 3, 0):
                 e2, kind2 = lax.rem(edge[kind] + de, 4), (kind + de) % 2
                 ty, tx = tile_place(e2, kind2, block, last)
                 for dg in range(groups):
@@ -402,28 +402,42 @@
         return packs[rnd].at[head_pack[kind] if which == 1 else tail_pack[kind]]
 
     def rim_slot(rnd, kind, which, e2, g2):
-        if which == 0:
-            return got_rim[rnd][kind].at[e2, g2], sem_r_rim.at[rnd, kind, e2, g2]
-        return got_end[rnd][kind].at[which - 1, e2, g2], sem_r_end.at[rnd, kind, which - 1, e2, g2]
+        at = e2 * groups + g2
+        return got_rim[rnd][kind].at[at] if which == 0 else got_end[rnd][kind].at[which - 1, at]
+
+    def rim_shared(rnd, kind, which):
+        shared = pl.ds(0, 4 * groups - (2 if which == 0 else 1))
+        return got_rim[rnd][kind].at[shared] if which == 0 else got_end[rnd][kind].at[which - 1, shared]
 
     def rim_sent(kind, which, de, dg):
-        return sem_s_rim.at[kind, de, dg] if which == 0 else sem_s_end.at[kind, which - 1, de, dg]
+        return pick(sem_s_rim.at[kind, which], sem_s_own.at[kind, which], which, de, dg)
+
+    def rim_got(rnd, kind, which, de, dg):
+        return pick(sem_r_rim.at[rnd, kind, which], sem_r_own.at[rnd, kind, which], which, de, dg)
+
+    def pick(shared, own, which, de, dg):
+        if dg or not (de in (1, 3) if which == 0 else de == 0):
+            return shared
+        return own.at[de // 2]
+
+    def rim_copy(rnd, kind, which, src, dst, de, dg, kind2, back, device):
+        return pltpu.make_async_remote_copy(
+            src_ref=src,
+            dst_ref=dst,
+            send_sem=rim_sent(kind, which, de, dg),
+            recv_sem=rim_got(rnd, kind2, which, back, dg),
+            device_id=device,
+            device_id_type=MESH,
+        )
 
     def rim_send(rnd, kind, which):
         src = rim_source(rnd, kind, which)
 
         def visit(de, dg, e2, kind2, g2, target, mine):
-            dst, recv = rim_slot(rnd, kind2, which, edge[kind], g)
+            dst = rim_slot(rnd, kind2, which, edge[kind], g)
 
             def there():
-                pltpu.make_async_remote_copy(
-                    src_ref=src,
-                    dst_ref=dst,
-                    send_sem=rim_sent(kind, which, de, dg),
-                    recv_sem=recv,
-                    device_id=target,
-                    device_id_type=MESH,
-                ).start()
+                rim_copy(rnd, kind, which, src, dst, de, dg, kind2, (4 - de) % 4, target).start()
 
             def here():
                 dst[...] = src[...]
@@ -432,43 +446,30 @@
 
         each_rim(kind, which, visit)
 
+    def rim_waits(rnd, kind, which, received):
+        first = []
+
+        def visit(de, dg, e2, kind2, g2, device, mine):
+            whole = mine is None
+            if whole and first:
+                return
+            if whole:
+                first.append(de)
+            ref = rim_shared(rnd, kind, which) if whole else rim_slot(rnd, kind, which, e2, g2)
+
+            def there():
+                copy = rim_copy(rnd, kind, which, ref, ref, de, dg, kind, de, device)
+                copy.wait_recv() if received else copy.wait_send()
+
+            sides(mine, None, there)
+
+        each_rim(kind, which, visit)
+
+    def rim_wait(rnd, kind, which):
+        rim_waits(rnd, kind, which, True)
+
     def rim_wait_send(rnd, kind, which):
-        src = rim_source(rnd, kind, which)
-
-        def visit(de, dg, e2, kind2, g2, target, mine):
-            dst, recv = rim_slot(rnd, kind2, which, edge[kind], g)
-
-            def there():
-                pltpu.make_async_remote_copy(
-                    src_ref=src,
-                    dst_ref=dst,
-                    send_sem=rim_sent(kind, which, de, dg),
-                    recv_sem=recv,
-                    device_id=target,
-                    device_id_type=MESH,
-                ).wait_send()
-
-            sides(mine, None, there)
-
-        each_rim(kind, which, visit)
-
-    def rim_wait(rnd, kind, which):
-        def visit(de, dg, e2, kind2, g2, source, mine):
-            dst, recv = rim_slot(rnd, kind, which, e2, g2)
-
-            def there():
-                pltpu.make_async_remote_copy(
-                    src_ref=dst,
-                    dst_ref=dst,
-                    send_sem=rim_sent(kind, which, de, dg),
-                    recv_sem=recv,
-                    device_id=source,
-                    device_id_type=MESH,
-                ).wait_recv()
-
-            sides(mine, None, there)
-
-        each_rim(kind, which, visit)
+        rim_waits(rnd, kind, which, False)
 
     sub = lax.broadcasted_iota(jnp.int32, (SIDE, 128), 0)
     lane = lax.broadcasted_iota(jnp.int32, (SIDE, 128), 1)
@@ -548,7 +549,7 @@
     def exchange(rnd):
         for n, (dy_, dx_) in enumerate(near):
             pl.when(has(dy_, dx_))(lambda n=n: near_copy(rnd, n).start())
-        for which in range(3):
+        for which in (1, 2, 0):
             for kind in range(2):
                 rim_send(rnd, kind, which)
 
@@ -603,10 +604,10 @@
                     turned = (1 + jnp.where(edge[kind] >= 2, 1, 0) + jnp.where(ne >= 2, 1, 0)) % 2
 
                     def partner(plane):
-                        v = got_rim[rnd][kind][ne, ng, plane]
+                        v = got_rim[rnd][kind][ne * groups + ng, plane]
                         v = jnp.where(turned == 1, mirror(v), v)
-                        head = wide_row(got_end[rnd][kind], 0, ne, ng, pl.ds(plane, 1))
-                        tail = wide_row(got_end[rnd][kind], 1, ne, ng, pl.ds(plane, 1))
+                        head = wide_row(got_end[rnd][kind], 0, ne * groups + ng, pl.ds(plane, 1))
+                        tail = wide_row(got_end[rnd][kind], 1, ne * groups + ng, pl.ds(plane, 1))
                         return v + jnp.where(
                             sub == first_at, head, jnp.where(sub == SIDE - 1 - first_at, tail, zero)
                         )
@@ -744,16 +745,16 @@
         + per_round((2,) + piece)
         + per_round((2,) + piece)
         + per_round((4, planes, 128))
-        + per_round((4, groups) + piece) * 2
-        + per_round((2, 4, groups, planes, 128)) * 2
+        + per_round((4 * groups,) + piece) * 2
+        + per_round((2, 4 * groups, planes, 128)) * 2
         + [pltpu.VMEM(tile, jnp.float32)] * 6
         + [
             pltpu.SemaphoreType.DMA((8,)),
             pltpu.SemaphoreType.DMA((ROUNDS, 8)),
-            pltpu.SemaphoreType.DMA((2, 4, groups)),
-            pltpu.SemaphoreType.DMA((ROUNDS, 2, 4, groups)),
-            pltpu.SemaphoreType.DMA((2, 2, 4, groups)),
-            pltpu.SemaphoreType.DMA((ROUNDS, 2, 2, 4, groups)),
+            pltpu.SemaphoreType.DMA((2, 3)),
+            pltpu.SemaphoreType.DMA((ROUNDS, 2, 3)),
+            pltpu.SemaphoreType.DMA((2, 3, 2)),
+            pltpu.SemaphoreType.DMA((ROUNDS, 2, 3, 2)),
         ]
     )
     vmem, smem = pl.BlockSpec(memory_space=pltpu.VMEM), pl.BlockSpec(memory_space=pltpu.SMEM)

time: 37.3 us -> 33.7 us (0.903)
  Pallas kernels: 35.5 us -> 32 us
    pallas_call x1, Pallas kernels: 35.5 us -> 32 us  [fused(): pl.pallas_call(functools.partial(kernel, groups, blocks), out_shape=jax.S...]
where the time goes in v3:
time: 33.7 us; the launch traced here: 33.6 us
  Pallas kernels  32 us (95%)
  local copies, waits for them, and re-layouts  1.62 us (5%)
    pallas_call x1, Pallas kernels, fused(): pl.pallas_call(functools.partial(kernel, groups, blocks), out_shape=jax.S...  32 us
    unnamed x1, local copies, waits for them, and re-layouts  1.62 us

profile of v3, /device:TPU:0, one launch (start us, length us, event | category | flops | bytes accessed | tf_op | source)
XLA Modules:
  0.0 33.6 jit_solution(3883315915052420298)
XLA Ops:
  0.0 32.0 %shard_map.73 = f32[3,8,8,192]{3,2,1,0:T(8,128)} custom-call(s32[4,6]{1,0:T(4,128)} %bitcast.2, s32[4,6]{1,0:T(4,128)} %bitcast.3, f32[3,8,8,192]{3,2,1,0:T(8,128)} %state.1, f32[3,8,8]{2,1,0:T(8,128)} %jac.1, f32[2,3,8,8]{3,2,1,0:T(8,128)} %diag.1, f32[3,8,8]{2,1,0:T(8,128)} %cross.1, f32[3,8,8]{2,1,0:T(8,128)} %coriolis.1), custom_call_target="tpu_custom_call" | custom-call | tf_op jit(solution)/shard_map/pallas_call | solution.py:761
  32.0 1.6 %copy.9 = f32[3,8,8,192]{3,2,1,0:T(8,128)} copy(f32[3,8,8,192]{3,2,1,0:T(8,128)} %shard_map.73) | data formatting | bytes 294912
